TPU v7x, 256 devices: a whole 4x4x8 slice. The times are simulated.
256 devices in a mesh: near: 16 (over y, x), row: 4 (over z_hi), col: 4 (over z_lo, core).
Axes of the slice: x: 4, y: 4, z: 8 (z_hi: 4, z_lo: 2; z = z_hi * 2 + z_lo), core: 2. Of those that a mesh axis runs over, the one named last changes fastest.
Arguments:
- right_side: float32 [256, 512, 128], P(('near', 'row', 'col')), may hold values from -6 to 6
- start_guess: float32 [256, 512, 128], P(('near', 'row', 'col')), may hold values from -6 to 6
- near_tiles: bfloat16 [256, 7, 512, 512], P(('near', 'row', 'col')), may hold values from -0.09375 to 0.09375
- tile_scales: float32 [256, 7], P(('near', 'row', 'col')), may hold values from 0.3 to 3
- neighbours: int32 [256, 7], P(('near', 'row', 'col')), may hold values from 0 to 255, as said below
- source_cluster_basis: bfloat16 [256, 512, 64], P(('near', 'row', 'col')), may hold values from -0.25 to 0.25
- basis_out: bfloat16 [256, 512, 64], P(('near', 'row', 'col')), may hold values from -0.75 to 0.75
- couplings: bfloat16 [256, 256, 64, 64], P(('near', 'row'), 'col'), may hold values from -0.046875 to 0.046875
Outputs:
- solution_field: float32 [256, 512, 128], P(('near', 'row', 'col'))
- residual: float32 [256, 512, 128], P(('near', 'row', 'col'))
Inputs may be any that keep to these rules, and one draw needn't show every extreme that they name: `neighbours`: row t names 7 different clusters, each within 4 of t in the wrapped cluster order.
All inputs are finite; a program needn't handle non-finite values.
Results may differ from a plain program's by a relative error of at most 0.0051.
Values may be sent and summed in bfloat16 or wider, within the bound.
No kernel may reach another device: no remote copies, remote signals or barrier semaphores. Data moves between devices by JAX's collectives and lax.ppermute only.
A program may use at most 64 MiB of HBM per device.

v0:
```python
import jax
import jax.numpy as jnp
from jax import lax
from jax.sharding import PartitionSpec as P

REACH = 4
ITERS = 2


damping = 0.5


def shifted(value, axis, steps):
    count = lax.axis_size(axis)
    pairs = [(source, (source + steps) % count) for source in range(count)]
    return lax.ppermute(value, axis, pairs)


def laid_out(blocks, dim):
    blocks = jnp.moveaxis(blocks, 0, dim)
    dims = blocks.shape
    return blocks.reshape(*dims[:dim], dims[dim] * dims[dim + 1], *dims[dim + 2 :])


def sent_to_all(array, axis):
    copies = jnp.broadcast_to(array, (lax.axis_size(axis), *array.shape))
    return lax.all_to_all(copies, axis, split_axis=0, concat_axis=0, tiled=True)


def collect(array, axis, dim):
    return laid_out(sent_to_all(array, axis), dim)


def in_blocks(array, dim, length):
    dims = array.shape
    blocks = array.reshape(*dims[:dim], length, dims[dim] // length, *dims[dim + 1 :])
    return jnp.moveaxis(blocks, dim, 0)


def summed_on_arrival(array, axis, dim):
    length = lax.axis_size(axis)
    blocks = lax.all_to_all(in_blocks(array, dim, length), axis, 0, 0, tiled=True)
    return jnp.sum(blocks, axis=0)


def shards(
    right_side,
    start_guess,
    near_tiles,
    tile_scales,
    neighbours,
    source_cluster_basis,
    basis_out,
    couplings,
):
    local_count = right_side.shape[0]
    clusters = local_count * lax.axis_size(("near", "row", "col"))
    col_count = lax.axis_size("col")
    col_index = lax.axis_index("col")
    group_index = lax.axis_index(("near", "row"))
    device = lax.axis_index(("near", "row", "col"))
    shift_count = REACH // local_count
    anchor_cluster = device * local_count + jnp.arange(local_count, dtype=jnp.int32)
    offsets = jnp.mod(neighbours - anchor_cluster[:, None] + REACH, clusters) - REACH
    window_rows = (jnp.arange(local_count, dtype=jnp.int32)[:, None] + REACH + offsets).reshape(-1)
    block_targets = group_index * couplings.shape[0] + jnp.arange(
        couplings.shape[0], dtype=jnp.int32
    )
    block_slots = col_index * couplings.shape[1] + jnp.arange(couplings.shape[1], dtype=jnp.int32)
    per_col = clusters // col_count
    within = block_slots % per_col
    column = block_slots // per_col
    distance = jnp.mod(
        block_targets[:, None]
        - ((within // local_count * col_count + column) * local_count + within % local_count)[
            None, :
        ],
        clusters,
    )
    admitted = (jnp.minimum(distance, clusters - distance) > REACH).astype(jnp.bfloat16)
    masked_values = couplings * admitted[:, :, None, None]
    iterate = start_guess
    residual = right_side
    for sweep in range(ITERS):
        coarse_level = iterate.astype(jnp.bfloat16)
        pieces = [coarse_level]
        for operate_distance in range(1, shift_count + 1):
            lower_part = shifted(coarse_level, ("near", "row", "col"), operate_distance)
            upper_part = shifted(coarse_level, ("near", "row", "col"), -operate_distance)
            pieces = [lower_part] + pieces + [upper_part]
        extended = jnp.concatenate(pieces, axis=0)
        nearby = jnp.take(extended, window_rows, axis=0).reshape(
            (local_count, near_tiles.shape[1]) + coarse_level.shape[1:]
        )
        basis_products = jnp.einsum(
            "ijkl,ijlc->ijkc", near_tiles, nearby, preferred_element_type=jnp.float32
        )
        near_term = jnp.sum(basis_products * tile_scales[:, :, None, None], axis=1)
        expansion_coefficients = jnp.einsum(
            "ilr,ilc->irc", source_cluster_basis, coarse_level, preferred_element_type=jnp.float32
        ).astype(jnp.bfloat16)
        partial_coefs = jnp.einsum(
            "lqsx,qxp->lsp",
            masked_values,
            collect(expansion_coefficients, ("near", "row"), 0),
            preferred_element_type=jnp.float32,
        )
        farfield_coefficients = summed_on_arrival(partial_coefs, "col", 0)
        far_term = jnp.einsum(
            "ila,iac->ilc",
            basis_out,
            farfield_coefficients.astype(jnp.bfloat16),
            preferred_element_type=jnp.float32,
        )
        residual = right_side - (iterate + near_term + far_term)
        iterate = iterate + damping * residual
    return (iterate, residual)


def solution(mesh):
    in_specs = (
        P(("near", "row", "col"), None, None),
        P(("near", "row", "col"), None, None),
        P(("near", "row", "col"), None, None, None),
        P(("near", "row", "col"), None),
        P(("near", "row", "col"), None),
        P(("near", "row", "col"), None, None),
        P(("near", "row", "col"), None, None),
        P(("near", "row"), "col", None, None),
    )
    out_specs = (P(("near", "row", "col"), None, None), P(("near", "row", "col"), None, None))
    return jax.shard_map(shards, mesh=mesh, in_specs=in_specs, out_specs=out_specs, check_vma=False)
```

profile of v0, /device:TPU:1, one launch (start us, length us, event | category | flops | bytes accessed | tf_op | source)
XLA Modules:
  0.0 168.3 jit_solution(9229464788245374934)
XLA Ops:
  0.6 0.0 copy-start
  0.6 1.0 convert_element_type.44
  1.6 1.0 convolution_convert_fusion.1
  2.6 1.3 broadcast_in_dim.20
  3.9 15.2 %all-to-all-start = ((bf16[64,1,64,128]{3,2,1,0:T(8,128)(2,1)}), bf16[64,1,64,128]{3,2,1,0:T(8,128)(2,1)S(1)}, u32[]{:S(2)}, u32[]{:S(2)}) async-start(bf16[64,1,64,128]{3,2,1,0:T(8,128)(2,1)} %broadcast_in_dim.20), calls=%async_computation | async-start | bytes 2097152 | tf_op jit(solution)/shard_map/all_to_all | solution.py:27
  19.1 2.0 %collective-permute-start = (bf16[1,512,128]{2,1,0:T(8,128)(2,1)S(1)}, bf16[1,512,128]{2,1,0:T(8,128)(2,1)S(1)}, u32[]{:S(2)}, u32[]{:S(2)}) collective-permute-start(bf16[1,512,128]{2,1,0:T(8,128)(2,1)S(1)} %convert_element_type.44), channel_id=1, source_target_pairs={{0,4},{1,5},{2,6},{3,7},{4,8},{5,9},{6,10},{7,11},{8,12},{9,13},{1... | collective-permute-start | bytes 393224 | tf_op jit(solution)/shard_map/ppermute | solution.py:16
  21.1 4.7 %collective-permute-start.1 = (bf16[1,512,128]{2,1,0:T(8,128)(2,1)S(1)}, bf16[1,512,128]{2,1,0:T(8,128)(2,1)}, u32[]{:S(2)}, u32[]{:S(2)}) collective-permute-start(bf16[1,512,128]{2,1,0:T(8,128)(2,1)S(1)} %convert_element_type.44), channel_id=1, source_target_pairs={{0,3},{1,4},{2,5},{3,6},{4,7},{5,8},{6,9},{7,10},{8,11},{9,12},{10... | collective-permute-start | bytes 393224 | tf_op jit(solution)/shard_map/ppermute | solution.py:16
  25.8 0.7 collective-permute-start.2
  26.6 0.0 collective-permute-start.3
  26.6 0.5 collective-permute-start.4
  27.1 0.1 fusion.45
  27.2 0.1 copy.21
  27.4 0.1 copy.20
  27.5 23.1 %collective-permute-done = bf16[1,512,128]{2,1,0:T(8,128)(2,1)S(1)} collective-permute-done((bf16[1,512,128]{2,1,0:T(8,128)(2,1)S(1)}, bf16[1,512,128]{2,1,0:T(8,128)(2,1)S(1)}, u32[]{:S(2)}, u32[]{:S(2)}) %collective-permute-start) | collective-permute-done | bytes 131104 | tf_op jit(solution)/shard_map/ppermute | solution.py:16
  50.6 0.7 copy-done.6
  51.3 7.5 %collective-permute-start.5 = (bf16[1,512,128]{2,1,0:T(8,128)(2,1)S(1)}, bf16[1,512,128]{2,1,0:T(8,128)(2,1)S(1)}, u32[]{:S(2)}, u32[]{:S(2)}) collective-permute-start(bf16[1,512,128]{2,1,0:T(8,128)(2,1)S(1)} %convert_element_type.44), channel_id=1, source_target_pairs={{0,254},{1,255},{2,0},{3,1},{4,2},{5,3},{6,4},{7,5},{8,6},{9,7},{1... | collective-permute-start | bytes 393224 | tf_op jit(solution)/shard_map/ppermute | solution.py:16
  58.8 0.9 constant_dynamic-update-slice_fusion.8
  59.7 0.4 collective-permute-done.1
  60.1 1.6 collective-permute-start.6
  61.6 0.9 constant_dynamic-update-slice_fusion.7
  62.6 0.0 collective-permute-done.2
  62.6 1.6 collective-permute-start.7
  64.2 0.9 constant_dynamic-update-slice_fusion.6
  65.1 0.0 collective-permute-done.3
  65.2 0.0 collective-permute-done.4
  65.2 0.0 collective-permute-done.5
  65.2 3.8 %collective-permute-done.6 = bf16[1,512,128]{2,1,0:T(8,128)(2,1)S(1)} collective-permute-done((bf16[1,512,128]{2,1,0:T(8,128)(2,1)S(1)}, bf16[1,512,128]{2,1,0:T(8,128)(2,1)S(1)}, u32[]{:S(2)}, u32[]{:S(2)}) %collective-permute-start.6) | collective-permute-done | bytes 131104 | tf_op jit(solution)/shard_map/ppermute | solution.py:16
  69.1 1.4 collective-permute-done.7
  70.5 1.6 gather_fusion
  72.1 0.0 all-to-all-done
  72.1 4.4 %fusion.20 = f32[4,1,64,128]{3,2,1,0:T(8,128)} fusion(bf16[4,64,64,64]{3,2,1,0:T(8,128)(2,1)} %param.17, bf16[4,64]{1,0:T(4,128)(2,1)S(1)} %fusion.45, bf16[64,1,64,128]{3,2,1,0:T(8,128)(2,1)S(1)} %all-to-all-done), kind=kOutput, calls=%fused_computation.22 | convolution fusion | flops 269484032 | bytes 3277312 | tf_op jit(solution)/shard_map/lqsx,qxp->lsp/dot_general | solution.py:102
  76.5 7.1 %all-to-all-start.1 = ((f32[4,1,64,128]{3,2,1,0:T(8,128)}), f32[4,1,64,128]{3,2,1,0:T(8,128)S(1)}, u32[]{:S(2)}, u32[]{:S(2)}) async-start(f32[4,1,64,128]{3,2,1,0:T(8,128)} %fusion.20), calls=%async_computation.1 | async-start | bytes 262144 | tf_op jit(solution)/shard_map/all_to_all | solution.py:42
  83.6 3.5 %multiply_reduce_fusion.1 = f32[128,512]{1,0:T(8,128)S(1)} fusion(bf16[1,7,512,512]{3,2,1,0:T(8,128)(2,1)} %param.12, bf16[7,512,128]{2,1,0:T(8,128)(2,1)S(1)} %copy-done.3, f32[7]{0:T(128)S(1)} %bitcast.91, pred[7]{0:T(512)(128)(4,1)S(1)} %get-tuple-element.7), kind=kOutput, calls=%fused_computation.13 | convolution fusion | flops 471072768 | bytes 4849699 | tf_op jit(solution)/shard_map/ijkl,ijlc->ijkc/dot_general | solution.py:95
  87.1 0.0 copy-start.5
  87.1 0.1 all-to-all-done.1
  87.2 0.2 fusion.52
  87.5 0.5 copy-done.5
  87.9 0.2 fusion.26
  88.1 1.2 broadcast_in_dim.21
  89.4 9.3 %all-to-all-start.2 = ((bf16[64,1,64,128]{3,2,1,0:T(8,128)(2,1)}), bf16[64,1,64,128]{3,2,1,0:T(8,128)(2,1)S(1)}, u32[]{:S(2)}, u32[]{:S(2)}) async-start(bf16[64,1,64,128]{3,2,1,0:T(8,128)(2,1)} %broadcast_in_dim.21), calls=%async_computation.2 | async-start | bytes 2097152 | tf_op jit(solution)/shard_map/all_to_all | solution.py:27
  98.7 2.2 %collective-permute-start.8 = (bf16[1,512,128]{1,2,0:T(8,128)(2,1)S(1)}, bf16[1,512,128]{1,2,0:T(8,128)(2,1)S(1)}, u32[]{:S(2)}, u32[]{:S(2)}) collective-permute-start(bf16[1,512,128]{1,2,0:T(8,128)(2,1)S(1)} %get-tuple-element.9), channel_id=1, source_target_pairs={{0,4},{1,5},{2,6},{3,7},{4,8},{5,9},{6,10},{7,11},{8,12},{9,13},{1... | collective-permute-start | bytes 393224 | tf_op jit(solution)/shard_map/ppermute | solution.py:16
  100.8 4.6 %collective-permute-start.9 = (bf16[1,512,128]{1,2,0:T(8,128)(2,1)S(1)}, bf16[1,512,128]{1,2,0:T(8,128)(2,1)S(1)}, u32[]{:S(2)}, u32[]{:S(2)}) collective-permute-start(bf16[1,512,128]{1,2,0:T(8,128)(2,1)S(1)} %get-tuple-element.9), channel_id=1, source_target_pairs={{0,3},{1,4},{2,5},{3,6},{4,7},{5,8},{6,9},{7,10},{8,11},{9,12},{10... | collective-permute-start | bytes 393224 | tf_op jit(solution)/shard_map/ppermute | solution.py:16
  105.4 1.2 collective-permute-start.10
  106.6 0.0 collective-permute-start.11
  106.6 0.5 collective-permute-start.12
  107.1 18.7 %collective-permute-done.8 = bf16[1,512,128]{1,2,0:T(8,128)(2,1)S(1)} collective-permute-done((bf16[1,512,128]{1,2,0:T(8,128)(2,1)S(1)}, bf16[1,512,128]{1,2,0:T(8,128)(2,1)S(1)}, u32[]{:S(2)}, u32[]{:S(2)}) %collective-permute-start.8) | collective-permute-done | bytes 131104 | tf_op jit(solution)/shard_map/ppermute | solution.py:16
  125.8 12.6 %collective-permute-start.13 = (bf16[1,512,128]{1,2,0:T(8,128)(2,1)S(1)}, bf16[1,512,128]{1,2,0:T(8,128)(2,1)S(1)}, u32[]{:S(2)}, u32[]{:S(2)}) collective-permute-start(bf16[1,512,128]{1,2,0:T(8,128)(2,1)S(1)} %get-tuple-element.9), channel_id=1, source_target_pairs={{0,254},{1,255},{2,0},{3,1},{4,2},{5,3},{6,4},{7,5},{8,6},{9,7},{1... | collective-permute-start | bytes 393224 | tf_op jit(solution)/shard_map/ppermute | solution.py:16
  138.5 1.1 collective-permute-done.9
  139.6 2.4 %collective-permute-start.14 = (bf16[1,512,128]{1,2,0:T(8,128)(2,1)S(1)}, bf16[1,512,128]{1,2,0:T(8,128)(2,1)S(1)}, u32[]{:S(2)}, u32[]{:S(2)}) collective-permute-start(bf16[1,512,128]{1,2,0:T(8,128)(2,1)S(1)} %get-tuple-element.9), channel_id=1, source_target_pairs={{0,253},{1,254},{2,255},{3,0},{4,1},{5,2},{6,3},{7,4},{8,5},{9,6},... | collective-permute-start | bytes 393224 | tf_op jit(solution)/shard_map/ppermute | solution.py:16
  142.0 0.5 collective-permute-done.10
  142.5 2.0 %collective-permute-start.15 = (bf16[1,512,128]{1,2,0:T(8,128)(2,1)S(1)}, bf16[1,512,128]{1,2,0:T(8,128)(2,1)S(1)}, u32[]{:S(2)}, u32[]{:S(2)}) collective-permute-start(bf16[1,512,128]{1,2,0:T(8,128)(2,1)S(1)} %get-tuple-element.9), channel_id=1, source_target_pairs={{0,252},{1,253},{2,254},{3,255},{4,0},{5,1},{6,2},{7,3},{8,4},{9,5... | collective-permute-start | bytes 393224 | tf_op jit(solution)/shard_map/ppermute | solution.py:16
  144.5 0.0 collective-permute-done.11
  144.6 0.0 collective-permute-done.13
  144.6 4.8 %collective-permute-done.14 = bf16[1,512,128]{1,2,0:T(8,128)(2,1)S(1)} collective-permute-done((bf16[1,512,128]{1,2,0:T(8,128)(2,1)S(1)}, bf16[1,512,128]{1,2,0:T(8,128)(2,1)S(1)}, u32[]{:S(2)}, u32[]{:S(2)}) %collective-permute-start.14) | collective-permute-done | bytes 131104 | tf_op jit(solution)/shard_map/ppermute | solution.py:16
  149.4 3.0 %collective-permute-done.15 = bf16[1,512,128]{1,2,0:T(8,128)(2,1)S(1)} collective-permute-done((bf16[1,512,128]{1,2,0:T(8,128)(2,1)S(1)}, bf16[1,512,128]{1,2,0:T(8,128)(2,1)S(1)}, u32[]{:S(2)}, u32[]{:S(2)}) %collective-permute-start.15) | collective-permute-done | bytes 131104 | tf_op jit(solution)/shard_map/ppermute | solution.py:16
  152.4 1.6 gather_fusion.1
  154.0 0.0 all-to-all-done.2
  154.0 4.4 %fusion.23 = f32[4,1,64,128]{3,2,1,0:T(8,128)} fusion(bf16[4,64,64,64]{3,2,1,0:T(8,128)(2,1)} %param.17, bf16[4,64]{1,0:T(4,128)(2,1)S(1)} %fusion.45, bf16[64,1,64,128]{3,2,1,0:T(8,128)(2,1)S(1)} %all-to-all-done.2), kind=kOutput, calls=%fused_computation.23 | convolution fusion | flops 269484032 | bytes 3277312 | tf_op jit(solution)/shard_map/lqsx,qxp->lsp/dot_general | solution.py:102
  158.4 4.4 %all-to-all-start.3 = ((f32[4,1,64,128]{3,2,1,0:T(8,128)}), f32[4,1,64,128]{3,2,1,0:T(8,128)S(1)}, u32[]{:S(2)}, u32[]{:S(2)}) async-start(f32[4,1,64,128]{3,2,1,0:T(8,128)} %fusion.23), calls=%async_computation.3 | async-start | bytes 262144 | tf_op jit(solution)/shard_map/all_to_all | solution.py:42
  162.8 3.4 %multiply_reduce_fusion = f32[128,512]{1,0:T(8,128)S(1)} fusion(bf16[1,7,512,512]{3,2,1,0:T(8,128)(2,1)} %param.12, bf16[7,512,128]{1,2,0:T(8,128)(2,1)S(1)} %copy-done.2, f32[7]{0:T(128)S(1)} %bitcast.92, pred[7]{0:T(512)(128)(4,1)S(1)} %get-tuple-element.7), kind=kOutput, calls=%fused_computation.12 | convolution fusion | flops 471072768 | bytes 4849699 | tf_op jit(solution)/shard_map/ijkl,ijlc->ijkc/dot_general | solution.py:95
  166.2 0.2 all-to-all-done.3
  166.4 0.2 multiply_add_fusion
  166.6 0.8 copy.24
  167.4 0.8 copy.25
  (36 shorter events, 0.3 us)
Async XLA Ops:
  0.6 86.6 %copy-start = (bf16[1,512,64]{1,2,0:T(8,128)(2,1)S(1)}, bf16[1,512,64]{1,2,0:T(8,128)(2,1)}, u32[]{:S(2)}) copy-start(bf16[1,512,64]{1,2,0:T(8,128)(2,1)} %param.16) | copy-start | bytes 196612
  3.9 23.3 %copy-start.7 = (s32[1,7]{1,0:T(1,128)S(1)}, s32[1,7]{1,0:T(1,128)}, u32[]{:S(2)}) copy-start(s32[1,7]{1,0:T(1,128)} %param.14) | copy-start | bytes 88
  3.9 23.3 %copy-start.1 = (f32[1,512,128]{2,1,0:T(8,128)S(1)}, f32[1,512,128]{2,1,0:T(8,128)}, u32[]{:S(2)}) copy-start(f32[1,512,128]{2,1,0:T(8,128)} %param.11) | copy-start | bytes 786436
  3.9 23.5 %copy-start.4 = (f32[1,512,128]{2,1,0:T(8,128)S(1)}, f32[1,512,128]{2,1,0:T(8,128)}, u32[]{:S(2)}) copy-start(f32[1,512,128]{2,1,0:T(8,128)} %param.10) | copy-start | bytes 786436
  3.9 68.2 %all-to-all-start = ((bf16[64,1,64,128]{3,2,1,0:T(8,128)(2,1)}), bf16[64,1,64,128]{3,2,1,0:T(8,128)(2,1)S(1)}, u32[]{:S(2)}, u32[]{:S(2)}) async-start(bf16[64,1,64,128]{3,2,1,0:T(8,128)(2,1)} %broadcast_in_dim.20), calls=%async_computation | async-start | bytes 2097152 | tf_op jit(solution)/shard_map/all_to_all | solution.py:27
  19.1 31.5 %collective-permute-start = (bf16[1,512,128]{2,1,0:T(8,128)(2,1)S(1)}, bf16[1,512,128]{2,1,0:T(8,128)(2,1)S(1)}, u32[]{:S(2)}, u32[]{:S(2)}) collective-permute-start(bf16[1,512,128]{2,1,0:T(8,128)(2,1)S(1)} %convert_element_type.44), channel_id=1, source_target_pairs={{0,4},{1,5},{2,6},{3,7},{4,8},{5,9},{6,10},{7,11},{8,12},{9,13},{1... | collective-permute-start | bytes 393224 | tf_op jit(solution)/shard_map/ppermute | solution.py:16
  21.1 39.0 %collective-permute-start.1 = (bf16[1,512,128]{2,1,0:T(8,128)(2,1)S(1)}, bf16[1,512,128]{2,1,0:T(8,128)(2,1)}, u32[]{:S(2)}, u32[]{:S(2)}) collective-permute-start(bf16[1,512,128]{2,1,0:T(8,128)(2,1)S(1)} %convert_element_type.44), channel_id=1, source_target_pairs={{0,3},{1,4},{2,5},{3,6},{4,7},{5,8},{6,9},{7,10},{8,11},{9,12},{10... | collective-permute-start | bytes 393224 | tf_op jit(solution)/shard_map/ppermute | solution.py:16
  25.8 36.8 %collective-permute-start.2 = (bf16[1,512,128]{2,1,0:T(8,128)(2,1)S(1)}, bf16[1,512,128]{2,1,0:T(8,128)(2,1)}, u32[]{:S(2)}, u32[]{:S(2)}) collective-permute-start(bf16[1,512,128]{2,1,0:T(8,128)(2,1)S(1)} %convert_element_type.44), channel_id=1, source_target_pairs={{0,2},{1,3},{2,4},{3,5},{4,6},{5,7},{6,8},{7,9},{8,10},{9,11},{10,... | collective-permute-start | bytes 393224 | tf_op jit(solution)/shard_map/ppermute | solution.py:16
  26.6 38.5 %collective-permute-start.3 = (bf16[1,512,128]{2,1,0:T(8,128)(2,1)S(1)}, bf16[1,512,128]{2,1,0:T(8,128)(2,1)S(1)}, u32[]{:S(2)}, u32[]{:S(2)}) collective-permute-start(bf16[1,512,128]{2,1,0:T(8,128)(2,1)S(1)} %convert_element_type.44), channel_id=1, source_target_pairs={{0,1},{1,2},{2,3},{3,4},{4,5},{5,6},{6,7},{7,8},{8,9},{9,10},{10,1... | collective-permute-start | bytes 393224 | tf_op jit(solution)/shard_map/ppermute | solution.py:16
  26.6 38.6 %collective-permute-start.4 = (bf16[1,512,128]{2,1,0:T(8,128)(2,1)S(1)}, bf16[1,512,128]{2,1,0:T(8,128)(2,1)S(1)}, u32[]{:S(2)}, u32[]{:S(2)}) collective-permute-start(bf16[1,512,128]{2,1,0:T(8,128)(2,1)S(1)} %convert_element_type.44), channel_id=1, source_target_pairs={{0,255},{1,0},{2,1},{3,2},{4,3},{5,4},{6,5},{7,6},{8,7},{9,8},{10,... | collective-permute-start | bytes 393224 | tf_op jit(solution)/shard_map/ppermute | solution.py:16
  50.6 0.7 copy-start.6
  51.3 13.9 %collective-permute-start.5 = (bf16[1,512,128]{2,1,0:T(8,128)(2,1)S(1)}, bf16[1,512,128]{2,1,0:T(8,128)(2,1)S(1)}, u32[]{:S(2)}, u32[]{:S(2)}) collective-permute-start(bf16[1,512,128]{2,1,0:T(8,128)(2,1)S(1)} %convert_element_type.44), channel_id=1, source_target_pairs={{0,254},{1,255},{2,0},{3,1},{4,2},{5,3},{6,4},{7,5},{8,6},{9,7},{1... | collective-permute-start | bytes 393224 | tf_op jit(solution)/shard_map/ppermute | solution.py:16
  60.1 9.0 %collective-permute-start.6 = (bf16[1,512,128]{2,1,0:T(8,128)(2,1)S(1)}, bf16[1,512,128]{2,1,0:T(8,128)(2,1)S(1)}, u32[]{:S(2)}, u32[]{:S(2)}) collective-permute-start(bf16[1,512,128]{2,1,0:T(8,128)(2,1)S(1)} %convert_element_type.44), channel_id=1, source_target_pairs={{0,253},{1,254},{2,255},{3,0},{4,1},{5,2},{6,3},{7,4},{8,5},{9,6},... | collective-permute-start | bytes 393224 | tf_op jit(solution)/shard_map/ppermute | solution.py:16
  62.6 7.9 %collective-permute-start.7 = (bf16[1,512,128]{2,1,0:T(8,128)(2,1)S(1)}, bf16[1,512,128]{2,1,0:T(8,128)(2,1)S(1)}, u32[]{:S(2)}, u32[]{:S(2)}) collective-permute-start(bf16[1,512,128]{2,1,0:T(8,128)(2,1)S(1)} %convert_element_type.44), channel_id=1, source_target_pairs={{0,252},{1,253},{2,254},{3,255},{4,0},{5,1},{6,2},{7,3},{8,4},{9,5... | collective-permute-start | bytes 393224 | tf_op jit(solution)/shard_map/ppermute | solution.py:16
  72.1 11.5 %copy-start.3 = (bf16[7,512,128]{2,1,0:T(8,128)(2,1)S(1)}, bf16[7,512,128]{2,1,0:T(8,128)(2,1)}, u32[]{:S(2)}) copy-start(bf16[7,512,128]{2,1,0:T(8,128)(2,1)} %gather_fusion) | copy-start | bytes 2752516
  72.1 11.5 %copy-start.8 = (f32[1,7]{1,0:T(1,128)S(1)}, f32[1,7]{1,0:T(1,128)}, u32[]{:S(2)}) copy-start(f32[1,7]{1,0:T(1,128)} %param.13) | copy-start | bytes 88
  76.5 10.7 %all-to-all-start.1 = ((f32[4,1,64,128]{3,2,1,0:T(8,128)}), f32[4,1,64,128]{3,2,1,0:T(8,128)S(1)}, u32[]{:S(2)}, u32[]{:S(2)}) async-start(f32[4,1,64,128]{3,2,1,0:T(8,128)} %fusion.20), calls=%async_computation.1 | async-start | bytes 262144 | tf_op jit(solution)/shard_map/all_to_all | solution.py:42
  87.1 0.8 copy-start.5
  89.4 64.6 %all-to-all-start.2 = ((bf16[64,1,64,128]{3,2,1,0:T(8,128)(2,1)}), bf16[64,1,64,128]{3,2,1,0:T(8,128)(2,1)S(1)}, u32[]{:S(2)}, u32[]{:S(2)}) async-start(bf16[64,1,64,128]{3,2,1,0:T(8,128)(2,1)} %broadcast_in_dim.21), calls=%async_computation.2 | async-start | bytes 2097152 | tf_op jit(solution)/shard_map/all_to_all | solution.py:27
  98.7 27.1 %collective-permute-start.8 = (bf16[1,512,128]{1,2,0:T(8,128)(2,1)S(1)}, bf16[1,512,128]{1,2,0:T(8,128)(2,1)S(1)}, u32[]{:S(2)}, u32[]{:S(2)}) collective-permute-start(bf16[1,512,128]{1,2,0:T(8,128)(2,1)S(1)} %get-tuple-element.9), channel_id=1, source_target_pairs={{0,4},{1,5},{2,6},{3,7},{4,8},{5,9},{6,10},{7,11},{8,12},{9,13},{1... | collective-permute-start | bytes 393224 | tf_op jit(solution)/shard_map/ppermute | solution.py:16
  100.8 38.7 %collective-permute-start.9 = (bf16[1,512,128]{1,2,0:T(8,128)(2,1)S(1)}, bf16[1,512,128]{1,2,0:T(8,128)(2,1)S(1)}, u32[]{:S(2)}, u32[]{:S(2)}) collective-permute-start(bf16[1,512,128]{1,2,0:T(8,128)(2,1)S(1)} %get-tuple-element.9), channel_id=1, source_target_pairs={{0,3},{1,4},{2,5},{3,6},{4,7},{5,8},{6,9},{7,10},{8,11},{9,12},{10... | collective-permute-start | bytes 393224 | tf_op jit(solution)/shard_map/ppermute | solution.py:16
  105.4 37.0 %collective-permute-start.10 = (bf16[1,512,128]{1,2,0:T(8,128)(2,1)S(1)}, bf16[1,512,128]{1,2,0:T(8,128)(2,1)S(1)}, u32[]{:S(2)}, u32[]{:S(2)}) collective-permute-start(bf16[1,512,128]{1,2,0:T(8,128)(2,1)S(1)} %get-tuple-element.9), channel_id=1, source_target_pairs={{0,2},{1,3},{2,4},{3,5},{4,6},{5,7},{6,8},{7,9},{8,10},{9,11},{10,... | collective-permute-start | bytes 393224 | tf_op jit(solution)/shard_map/ppermute | solution.py:16
  106.6 37.9 %collective-permute-start.11 = (bf16[1,512,128]{1,2,0:T(8,128)(2,1)S(1)}, bf16[1,512,128]{1,2,0:T(8,128)(2,1)S(1)}, u32[]{:S(2)}, u32[]{:S(2)}) collective-permute-start(bf16[1,512,128]{1,2,0:T(8,128)(2,1)S(1)} %get-tuple-element.9), channel_id=1, source_target_pairs={{0,1},{1,2},{2,3},{3,4},{4,5},{5,6},{6,7},{7,8},{8,9},{9,10},{10,1... | collective-permute-start | bytes 393224 | tf_op jit(solution)/shard_map/ppermute | solution.py:16
  106.6 37.9 %collective-permute-start.12 = (bf16[1,512,128]{1,2,0:T(8,128)(2,1)S(1)}, bf16[1,512,128]{1,2,0:T(8,128)(2,1)S(1)}, u32[]{:S(2)}, u32[]{:S(2)}) collective-permute-start(bf16[1,512,128]{1,2,0:T(8,128)(2,1)S(1)} %get-tuple-element.9), channel_id=1, source_target_pairs={{0,255},{1,0},{2,1},{3,2},{4,3},{5,4},{6,5},{7,6},{8,7},{9,8},{10,... | collective-permute-start | bytes 393224 | tf_op jit(solution)/shard_map/ppermute | solution.py:16
  125.8 18.8 %collective-permute-start.13 = (bf16[1,512,128]{1,2,0:T(8,128)(2,1)S(1)}, bf16[1,512,128]{1,2,0:T(8,128)(2,1)S(1)}, u32[]{:S(2)}, u32[]{:S(2)}) collective-permute-start(bf16[1,512,128]{1,2,0:T(8,128)(2,1)S(1)} %get-tuple-element.9), channel_id=1, source_target_pairs={{0,254},{1,255},{2,0},{3,1},{4,2},{5,3},{6,4},{7,5},{8,6},{9,7},{1... | collective-permute-start | bytes 393224 | tf_op jit(solution)/shard_map/ppermute | solution.py:16
  139.6 9.8 %collective-permute-start.14 = (bf16[1,512,128]{1,2,0:T(8,128)(2,1)S(1)}, bf16[1,512,128]{1,2,0:T(8,128)(2,1)S(1)}, u32[]{:S(2)}, u32[]{:S(2)}) collective-permute-start(bf16[1,512,128]{1,2,0:T(8,128)(2,1)S(1)} %get-tuple-element.9), channel_id=1, source_target_pairs={{0,253},{1,254},{2,255},{3,0},{4,1},{5,2},{6,3},{7,4},{8,5},{9,6},... | collective-permute-start | bytes 393224 | tf_op jit(solution)/shard_map/ppermute | solution.py:16
  142.5 9.9 %collective-permute-start.15 = (bf16[1,512,128]{1,2,0:T(8,128)(2,1)S(1)}, bf16[1,512,128]{1,2,0:T(8,128)(2,1)S(1)}, u32[]{:S(2)}, u32[]{:S(2)}) collective-permute-start(bf16[1,512,128]{1,2,0:T(8,128)(2,1)S(1)} %get-tuple-element.9), channel_id=1, source_target_pairs={{0,252},{1,253},{2,254},{3,255},{4,0},{5,1},{6,2},{7,3},{8,4},{9,5... | collective-permute-start | bytes 393224 | tf_op jit(solution)/shard_map/ppermute | solution.py:16
  154.0 8.8 %copy-start.2 = (bf16[7,512,128]{1,2,0:T(8,128)(2,1)S(1)}, bf16[7,512,128]{1,2,0:T(8,128)(2,1)}, u32[]{:S(2)}) copy-start(bf16[7,512,128]{1,2,0:T(8,128)(2,1)} %gather_fusion.1) | copy-start | bytes 2752516
  158.4 8.0 %all-to-all-start.3 = ((f32[4,1,64,128]{3,2,1,0:T(8,128)}), f32[4,1,64,128]{3,2,1,0:T(8,128)S(1)}, u32[]{:S(2)}, u32[]{:S(2)}) async-start(f32[4,1,64,128]{3,2,1,0:T(8,128)} %fusion.23), calls=%async_computation.3 | async-start | bytes 262144 | tf_op jit(solution)/shard_map/all_to_all | solution.py:42
where the time goes:
time: 169 us; the launch traced here: 168 us
  starting transfers between devices  80.2 us (47%)
  waiting for transfers between devices  57.1 us (34%)
  matrix products  17.2 us (10%)
  local copies, waits for them, and re-layouts  11.7 us (7%)
    ppermute x16, waiting for transfers between devices, shifted(): return lax.ppermute(value, axis, pairs)  56.8 us
    ppermute x16, starting transfers between devices, shifted(): return lax.ppermute(value, axis, pairs)  44.1 us
    all_to_all x2, starting transfers between devices, sent_to_all(): return lax.all_to_all(copies, axis, split_axis=0, concat_axis=0, tiled=True)  24.5 us
    all_to_all x2, starting transfers between devices, summed_on_arrival(): lax.all_to_all(in_blocks(array, dim, length), axis, 0, 0, tiled=True)  11.5 us
    dot_general x2, matrix products, shards(): jnp.einsum('lqsx,qxp->lsp', masked_values, collect(expansion_coefficients...  8.76 us
    dot_general x2, matrix products, shards(): jnp.einsum('ijkl,ijlc->ijkc', near_tiles, nearby, preferred_element_type=...  6.84 us
    unnamed x37, local copies, waits for them, and re-layouts  6.02 us
  transfers between devices with their start and end apart: 20, of which 11 were waited for; matrix products, arithmetic and copies ran while one was open for 8% of the time, Pallas kernels for 0%

commit v1 on v0

v1 whole, which is shorter than its diff:
```python
import jax
import jax.numpy as jnp
from jax import lax
from jax.experimental import pallas as pl
from jax.experimental.pallas import tpu as pltpu
from jax.sharding import PartitionSpec as P

REACH = 4
ITERS = 2
ALL = ("near", "row", "col")

damping = 0.5

SLOTS = (8, 6, 7, 1, 0, 3, 2, 5, 4)


def moved(value, target):
    count = lax.axis_size(ALL)
    return lax.ppermute(value, ALL, [(source, target(source) % count) for source in range(count)])


def outward(steps):
    return lambda source: source + steps if source % 2 == 0 else source - steps


def partner(source):
    return source ^ 1


def sent_to_all(array, axis):
    copies = jnp.broadcast_to(array, (lax.axis_size(axis), *array.shape))
    return lax.all_to_all(copies, axis, split_axis=0, concat_axis=0, tiled=True)


def near_body(slots, scales, tiles, own, other, first, second, back, out, window):
    step = pl.program_id(0)

    @pl.when(step == 0)
    def _():
        window[0] = own[...]
        window[1] = other[...]
        window[2:4] = first[...]
        window[4:6] = second[...]
        window[6:9] = back[...]

    product = scales[step] * jnp.dot(
        tiles[0], window[slots[step]], preferred_element_type=jnp.float32
    )

    @pl.when(step == 0)
    def _():
        out[...] = product

    @pl.when(step > 0)
    def _():
        out[...] += product


def near_product(slots, scales, tiles, own, other, first, second, back):
    count, rows, inner = tiles.shape
    cols = own.shape[-1]

    def whole(array):
        return pl.BlockSpec(array.shape, lambda k, *_: (0,) * array.ndim)

    return pl.pallas_call(
        near_body,
        out_shape=jax.ShapeDtypeStruct((rows, cols), jnp.float32),
        grid_spec=pltpu.PrefetchScalarGridSpec(
            num_scalar_prefetch=2,
            grid=(count,),
            in_specs=[
                pl.BlockSpec((1, rows, inner), lambda k, *_: (k, 0, 0)),
                whole(own),
                whole(other),
                whole(first),
                whole(second),
                whole(back),
            ],
            out_specs=pl.BlockSpec((rows, cols), lambda k, *_: (0, 0)),
            scratch_shapes=[pltpu.VMEM((2 * REACH + 1, rows, cols), own.dtype)],
        ),
        cost_estimate=pl.CostEstimate(
            flops=2 * count * rows * inner * cols,
            bytes_accessed=2 * count * rows * inner,
            transcendentals=0,
        ),
        name="near",
    )(slots, scales, tiles, own, other, first, second, back)


def halo(own):
    other = moved(own, partner)
    pair = jnp.stack([own, other])
    first = moved(pair, outward(2))
    second = moved(pair, outward(4))
    back = moved(jnp.concatenate([first, second[1:]]), partner)
    return own, other, first, second, back


def shards(
    right_side,
    start_guess,
    near_tiles,
    tile_scales,
    neighbours,
    source_cluster_basis,
    basis_out,
    couplings,
):
    right_side, iterate = right_side[0], start_guess[0]
    near_tiles, scales = near_tiles[0], tile_scales[0]
    basis_in, basis_out = source_cluster_basis[0], basis_out[0]
    clusters = lax.axis_size(ALL)
    col_count = lax.axis_size("col")
    col_index = lax.axis_index("col")
    group_index = lax.axis_index(("near", "row"))
    device = lax.axis_index(ALL)
    side = 2 * (device % 2) - 1
    offsets = jnp.mod(neighbours[0] - device + REACH, clusters) - REACH
    places = jnp.arange(2 * REACH + 1, dtype=jnp.int32)
    chosen = (side * offsets + REACH)[:, None] == places[None, :]
    slots = jnp.sum(jnp.where(chosen, jnp.array(SLOTS, jnp.int32)[None, :], 0), axis=1)

    targets, sources, rank, _ = couplings.shape
    block_targets = group_index * targets + jnp.arange(targets, dtype=jnp.int32)
    block_sources = jnp.arange(sources, dtype=jnp.int32) * col_count + col_index
    distance = jnp.mod(block_targets[:, None] - block_sources[None, :], clusters)
    admitted = (jnp.minimum(distance, clusters - distance) > REACH).astype(couplings.dtype)
    masked = couplings * admitted[:, :, None, None]
    far_rows = jnp.transpose(masked, (0, 2, 1, 3)).reshape(targets * rank, sources * rank)
    far_rows = lax.optimization_barrier(far_rows)

    residual = right_side
    for sweep in range(ITERS):
        coarse = iterate.astype(jnp.bfloat16)
        coefs = jnp.einsum(
            "lr,lc->rc", basis_in, coarse, preferred_element_type=jnp.float32
        ).astype(jnp.bfloat16)
        gathered = sent_to_all(sent_to_all(coefs, "row"), "near")
        near_term = near_product(slots, scales, near_tiles, *halo(coarse))
        partial_coefs = jnp.dot(
            far_rows, gathered.reshape(sources * rank, -1), preferred_element_type=jnp.float32
        ).astype(jnp.bfloat16)
        pieces = lax.all_to_all(
            partial_coefs.reshape(targets, rank, -1), "col", 0, 0, tiled=True
        )
        far_coefs = jnp.sum(pieces.astype(jnp.float32), axis=0).astype(jnp.bfloat16)
        far_term = jnp.dot(basis_out, far_coefs, preferred_element_type=jnp.float32)
        residual = right_side - (iterate + near_term + far_term)
        iterate = iterate + damping * residual
    return (iterate[None], residual[None])


def solution(mesh):
    in_specs = (
        P(ALL, None, None),
        P(ALL, None, None),
        P(ALL, None, None, None),
        P(ALL, None),
        P(ALL, None),
        P(ALL, None, None),
        P(ALL, None, None),
        P(("near", "row"), "col", None, None),
    )
    out_specs = (P(ALL, None, None), P(ALL, None, None))
    return jax.shard_map(shards, mesh=mesh, in_specs=in_specs, out_specs=out_specs, check_vma=False)
```

time: 169 us -> 125 us (0.74)
  waiting for transfers between devices: 57.1 us -> 15.4 us
  starting transfers between devices: 80.2 us -> 47.9 us
  Pallas kernels: 0 us -> 14.7 us
  matrix products: 17.2 us -> 4.29 us
  blocking collectives: 0 us -> 11.3 us
  other arithmetic: 1.17 us -> 12.4 us
  local copies, waits for them, and re-layouts: 11.7 us -> 17.5 us
    ppermute x16 -> x8, waiting for transfers between devices: 56.8 us -> 9.31 us  [moved(): lax.ppermute(value, ALL, [(source, target(source) % count) for source in...]
    ppermute x16 -> x8, starting transfers between devices: 44.1 us -> 18.1 us  [moved(): lax.ppermute(value, ALL, [(source, target(source) % count) for source in...]
    pallas_call x0 -> x2, Pallas kernels: none -> 14.7 us  [near_product(): pl.pallas_call(near_body, out_shape=jax.ShapeDtypeStruct((rows, cols), jn...]
    dot_general x8 -> x6, matrix products: 17.2 us -> 4.29 us  [the longest x2 2.63 us: shards(): jnp.dot(far_rows, gathered.reshape(sources * rank, -1), preferred_element...]
    all_to_all x0 -> x1, blocking collectives: none -> 11.3 us  [sent_to_all(): return lax.all_to_all(copies, axis, split_axis=0, concat_axis=0, tiled=True)]
    transpose x0 -> x1, local copies, waits for them, and re-layouts: none -> 6.91 us  [shards(): jnp.transpose(masked, (0, 2, 1, 3)).reshape(targets * rank, sources * rank)]
    all_to_all x2 -> x3, waiting for transfers between devices: 0.01 us -> 6.08 us  [sent_to_all(): return lax.all_to_all(copies, axis, split_axis=0, concat_axis=0, tiled=True)]
    reshape x0 -> x1, local copies, waits for them, and re-layouts: none -> 5.68 us  [shards(): jnp.transpose(masked, (0, 2, 1, 3)).reshape(targets * rank, sources * rank)]
  transfers between devices with their start and end apart: 20 -> 13, of which waited for: 11 -> 4; matrix products, arithmetic and copies ran while one was open for 8% -> 20% of each run, Pallas kernels for 0% -> 12%
where the time goes in v1:
time: 125 us; the launch traced here: 124 us
  starting transfers between devices  47.9 us (38%)
  local copies, waits for them, and re-layouts  17.5 us (14%)
  waiting for transfers between devices  15.4 us (12%)
  Pallas kernels  14.7 us (12%)
  other arithmetic  12.4 us (10%)
  blocking collectives  11.3 us (9%)
  matrix products  4.29 us (3%)
    all_to_all x3, starting transfers between devices, sent_to_all(): return lax.all_to_all(copies, axis, split_axis=0, concat_axis=0, tiled=True)  21.9 us
    ppermute x8, starting transfers between devices, moved(): lax.ppermute(value, ALL, [(source, target(source) % count) for source in...  18.1 us
    pallas_call x2, Pallas kernels, near_product(): pl.pallas_call(near_body, out_shape=jax.ShapeDtypeStruct((rows, cols), jn...  14.7 us
    all_to_all x1, blocking collectives, sent_to_all(): return lax.all_to_all(copies, axis, split_axis=0, concat_axis=0, tiled=True)  11.3 us
    ppermute x8, waiting for transfers between devices, moved(): lax.ppermute(value, ALL, [(source, target(source) % count) for source in...  9.31 us
    all_to_all x2, starting transfers between devices, shards(): lax.all_to_all(partial_coefs.reshape(targets, rank, -1), 'col', 0, 0, til...  7.89 us
    transpose x1, local copies, waits for them, and re-layouts, shards(): jnp.transpose(masked, (0, 2, 1, 3)).reshape(targets * rank, sources * rank)  6.91 us
    all_to_all x3, waiting for transfers between devices, sent_to_all(): return lax.all_to_all(copies, axis, split_axis=0, concat_axis=0, tiled=True)  6.08 us
  transfers between devices with their start and end apart: 13, of which 4 were waited for; matrix products, arithmetic and copies ran while one was open for 20% of the time, Pallas kernels for 12%

profile of v1, /device:TPU:1, one launch (start us, length us, event | category | flops | bytes accessed | tf_op | source)
XLA Modules:
  0.0 124.4 jit_solution(8580556979441520671)
XLA Ops:
  0.6 0.0 copy-start
  0.6 1.1 bitcast_convert_fusion
  1.7 0.0 copy-start.9
  1.8 1.0 convolution_convert_fusion.3
  2.8 0.6 broadcast_in_dim.38
  3.4 9.0 %all-to-all-start = ((bf16[4,64,128]{2,1,0:T(8,128)(2,1)}), bf16[4,64,128]{2,1,0:T(8,128)(2,1)S(1)}, u32[]{:S(2)}, u32[]{:S(2)}) async-start(bf16[4,64,128]{2,1,0:T(8,128)(2,1)} %broadcast_in_dim.38), calls=%async_computation | async-start | bytes 131072 | tf_op jit(solution)/shard_map/all_to_all | solution.py:32
  12.4 1.0 collective-permute-start
  13.4 6.1 %all-to-all-done = bf16[4,64,128]{2,1,0:T(8,128)(2,1)S(1)} async-done(((bf16[4,64,128]{2,1,0:T(8,128)(2,1)}), bf16[4,64,128]{2,1,0:T(8,128)(2,1)S(1)}, u32[]{:S(2)}, u32[]{:S(2)}) %all-to-all-start) | async-done | bytes 65568 | tf_op jit(solution)/shard_map/all_to_all | solution.py:32
  19.5 1.3 %broadcast_in_dim.39 = bf16[16,4,64,128]{3,2,1,0:T(8,128)(2,1)} broadcast(bf16[4,64,128]{2,1,0:T(8,128)(2,1)S(1)} %all-to-all-done), dimensions={1,2,3} | broadcast | bytes 1114112 | tf_op jit(solution)/shard_map/broadcast_in_dim | solution.py:31
  20.8 6.8 %all-to-all-start.1 = ((bf16[16,4,64,128]{3,2,1,0:T(8,128)(2,1)}), bf16[16,4,64,128]{3,2,1,0:T(8,128)(2,1)S(1)}, u32[]{:S(2)}, u32[]{:S(2)}) async-start(bf16[16,4,64,128]{3,2,1,0:T(8,128)(2,1)} %broadcast_in_dim.39), calls=%async_computation.1 | async-start | bytes 2097152 | tf_op jit(solution)/shard_map/all_to_all | solution.py:32
  27.6 0.1 fusion.11
  27.7 0.0 collective-permute-done.other
  27.7 0.0 copy-start.10
  27.7 0.7 pad_maximum_fusion.2
  28.4 4.1 %collective-permute-start.1 = (bf16[2,512,128]{2,1,0:T(8,128)(2,1)}, bf16[2,512,128]{2,1,0:T(8,128)(2,1)S(1)}, u32[]{:S(2)}, u32[]{:S(2)}) collective-permute-start(bf16[2,512,128]{2,1,0:T(8,128)(2,1)} %pad_maximum_fusion.2), channel_id=1, source_target_pairs={{0,2},{1,255},{2,4},{3,1},{4,6},{5,3},{6,8},{7,5},{8,10},{9,7},{10... | collective-permute-start | bytes 786440 | tf_op jit(solution)/shard_map/ppermute | solution.py:19
  32.5 0.7 collective-permute-start.2
  33.2 4.5 %multiply_bitcast_fusion = bf16[4,64,64,64]{3,1,2,0:T(8,128)(2,1)} fusion(bf16[4,64,64,64]{3,2,1,0:T(8,128)(2,1)} %param.16, bf16[4,64]{1,0:T(4,128)(2,1)S(1)} %fusion.11), kind=kLoop, calls=%fused_computation | loop fusion | flops 1048576 | bytes 4194816 | tf_op jit(solution)/shard_map/transpose | solution.py:131
  37.7 0.0 copy-done.9
  37.7 0.0 copy-done.10
  37.7 6.9 %copy.16 = bf16[4,64,64,64]{3,2,1,0:T(8,128)(2,1)} copy(bf16[4,64,64,64]{3,1,2,0:T(8,128)(2,1)} %multiply_bitcast_fusion) | data formatting | bytes 4194304 | tf_op jit(solution)/shard_map/transpose | solution.py:131
  44.6 5.7 %reshape.96 = bf16[256,4096]{1,0:T(8,128)(2,1)S(1)} reshape(bf16[4,64,64,64]{3,2,1,0:T(8,128)(2,1)} %copy.16) | data formatting | bytes 4194304 | tf_op jit(solution)/shard_map/reshape | solution.py:131
  50.3 0.0 copy-start.14
  50.3 0.0 copy-done.13
  50.3 0.0 collective-permute-done.2.second
  50.3 0.9 slice.8
  51.2 0.0 collective-permute-done.1.first
  51.3 0.0 copy-start.2
  51.3 0.8 pad_maximum_fusion
  52.1 0.0 collective-permute-start.3
  52.1 0.0 all-to-all-done.1
  52.1 1.3 %convolution_convert_fusion.1 = bf16[256,128]{1,0:T(8,128)(2,1)} fusion(bf16[256,4096]{1,0:T(8,128)(2,1)S(1)} %reshape.96, bf16[4096,128]{1,0:T(8,128)(2,1)S(1)} %bitcast.68), kind=kOutput, calls=%fused_computation.4 | convolution fusion | flops 268468224 | bytes 3211264 | tf_op jit(solution)/shard_map/dot_general | solution.py:142
  53.4 3.9 %all-to-all-start.2 = ((bf16[4,64,128]{2,1,0:T(8,128)(2,1)}), bf16[4,64,128]{2,1,0:T(8,128)(2,1)S(1)}, u32[]{:S(2)}, u32[]{:S(2)}) async-start(bf16[4,64,128]{2,1,0:T(8,128)(2,1)} %bitcast.10), calls=%async_computation.2 | async-start | bytes 131072 | tf_op jit(solution)/shard_map/all_to_all | solution.py:145
  57.3 0.0 copy-done.14
  57.3 0.7 select_reduce_fusion.slots
  58.0 0.0 collective-permute-done.3.back
  58.0 0.0 copy-done.2
  58.0 7.4 %near.2 = f32[512,128]{1,0:T(8,128)} custom-call(s32[7]{0:T(128)} %select_reduce_fusion.slots, f32[7]{0:T(128)} %bitcast.73, bf16[7,512,512]{2,1,0:T(8,128)(2,1)} %bitcast.66, bf16[512,128]{1,0:T(8,128)(2,1)} %copy-done.9, bf16[512,128]{1,0:T(8,128)(2,1)} %copy-done.10, bf16[2,512,128]{2,1,0:T(8,128)(2,1)} %copy-done.2, ...), custom_call_target="tpu_custom_call" | custom-call | flops 469762048 | bytes 3670016 | tf_op jit(solution)/shard_map/near/pallas_call | solution.py:66
  65.4 0.0 all-to-all-done.2
  65.4 0.2 convolution_bitcast_fusion.1
  65.7 0.0 copy-done.4
  65.7 0.0 copy-done.5
  65.7 1.7 %fusion.17 = (bf16[512,128]{1,0:T(8,128)(2,1)S(1)}, f32[512,128]{1,0:T(8,128)}) fusion(f32[512,128]{1,0:T(8,128)S(1)} %convolution_bitcast_fusion.1, f32[512,128]{1,0:T(8,128)} %near.2, f32[1,512,128]{2,1,0:T(8,128)S(1)} %copy-done.5, f32[1,512,128]{2,1,0:T(8,128)S(1)} %copy-done.4), kind=kLoop, calls=%fused_computation.46 | loop fusion | flops 393216 | bytes 1441792 | tf_op jit(solution)/shard_map/convert_element_type | solution.py:136
  67.4 0.0 copy-done.12
  67.4 0.2 fusion
  67.6 11.3 %all_to_all.30 = bf16[4,64,128]{2,1,0:T(8,128)(2,1)S(1)} all-to-all(bf16[4,64,128]{2,1,0:T(8,128)(2,1)S(1)} %broadcast_in_dim.40), channel_id=1, replica_groups=mesh['near'=16,'row'=4,'col'=4] {'row'}, dimensions={0} | all-to-all | bytes 131072 | tf_op jit(solution)/shard_map/all_to_all | solution.py:32
  78.9 1.3 %broadcast_in_dim.41 = bf16[16,4,64,128]{3,2,1,0:T(8,128)(2,1)} broadcast(bf16[4,64,128]{2,1,0:T(8,128)(2,1)S(1)} %all_to_all.30), dimensions={1,2,3} | broadcast | bytes 1114112 | tf_op jit(solution)/shard_map/broadcast_in_dim | solution.py:31
  80.2 6.2 %all-to-all-start.4 = ((bf16[16,4,64,128]{3,2,1,0:T(8,128)(2,1)}), bf16[16,4,64,128]{3,2,1,0:T(8,128)(2,1)S(1)}, u32[]{:S(2)}, u32[]{:S(2)}) async-start(bf16[16,4,64,128]{3,2,1,0:T(8,128)(2,1)} %broadcast_in_dim.41), calls=%async_computation.4 | async-start | bytes 2097152 | tf_op jit(solution)/shard_map/all_to_all | solution.py:32
  86.4 2.3 %collective-permute-start.4 = (bf16[512,128]{1,0:T(8,128)(2,1)S(1)}, bf16[512,128]{1,0:T(8,128)(2,1)S(1)}, u32[]{:S(2)}, u32[]{:S(2)}) collective-permute-start(bf16[512,128]{1,0:T(8,128)(2,1)S(1)} %get-tuple-element.2.own), channel_id=1, source_target_pairs={{0,1},{1,0},{2,3},{3,2},{4,5},{5,4},{6,7},{7,6},{8,9},{9,8},{10,11... | collective-permute-start | bytes 393224 | tf_op jit(solution)/shard_map/ppermute | solution.py:19
  88.7 1.0 collective-permute-done.4.other
  89.7 4.6 %collective-permute-start.6 = (bf16[2,512,128]{2,1,0:T(8,128)(2,1)S(1)}, bf16[2,512,128]{2,1,0:T(8,128)(2,1)S(1)}, u32[]{:S(2)}, u32[]{:S(2)}) collective-permute-start(bf16[2,512,128]{2,1,0:T(8,128)(2,1)S(1)} %pad_maximum_fusion.3), channel_id=1, source_target_pairs={{0,4},{1,253},{2,6},{3,255},{4,8},{5,1},{6,10},{7,3},{8,12},{9,5},... | collective-permute-start | bytes 786440 | tf_op jit(solution)/shard_map/ppermute | solution.py:19
  94.4 0.5 collective-permute-start.5
  94.8 5.7 %collective-permute-done.6.second = bf16[2,512,128]{2,1,0:T(8,128)(2,1)S(1)} collective-permute-done((bf16[2,512,128]{2,1,0:T(8,128)(2,1)S(1)}, bf16[2,512,128]{2,1,0:T(8,128)(2,1)S(1)}, u32[]{:S(2)}, u32[]{:S(2)}) %collective-permute-start.6) | collective-permute-done | bytes 262176 | tf_op jit(solution)/shard_map/ppermute | solution.py:19
  100.5 0.7 copy-done.8
  101.2 2.6 %collective-permute-done.5.first = bf16[2,512,128]{2,1,0:T(8,128)(2,1)S(1)} collective-permute-done((bf16[2,512,128]{2,1,0:T(8,128)(2,1)S(1)}, bf16[2,512,128]{2,1,0:T(8,128)(2,1)S(1)}, u32[]{:S(2)}, u32[]{:S(2)}) %collective-permute-start.5) | collective-permute-done | bytes 262176 | tf_op jit(solution)/shard_map/ppermute | solution.py:19
  103.8 0.8 pad_maximum_fusion.1
  104.7 4.9 %collective-permute-start.7 = (bf16[3,512,128]{2,1,0:T(8,128)(2,1)}, bf16[3,512,128]{2,1,0:T(8,128)(2,1)}, u32[]{:S(2)}, u32[]{:S(2)}) collective-permute-start(bf16[3,512,128]{2,1,0:T(8,128)(2,1)} %pad_maximum_fusion.1), channel_id=1, source_target_pairs={{0,1},{1,0},{2,3},{3,2},{4,5},{5,4},{6,7},{7,6},{8,9},{9,8},{10,11... | collective-permute-start | bytes 1179656 | tf_op jit(solution)/shard_map/ppermute | solution.py:19
  109.6 0.0 all-to-all-done.4
  109.6 1.3 %convolution_convert_fusion = bf16[256,128]{1,0:T(8,128)(2,1)} fusion(bf16[256,4096]{1,0:T(8,128)(2,1)S(1)} %reshape.96, bf16[4096,128]{1,0:T(8,128)(2,1)S(1)} %bitcast.69), kind=kOutput, calls=%fused_computation.3 | convolution fusion | flops 268468224 | bytes 3211264 | tf_op jit(solution)/shard_map/dot_general | solution.py:142
  110.9 4.0 %all-to-all-start.5 = ((bf16[4,64,128]{2,1,0:T(8,128)(2,1)}), bf16[4,64,128]{2,1,0:T(8,128)(2,1)S(1)}, u32[]{:S(2)}, u32[]{:S(2)}) async-start(bf16[4,64,128]{2,1,0:T(8,128)(2,1)} %bitcast.17), calls=%async_computation.5 | async-start | bytes 131072 | tf_op jit(solution)/shard_map/all_to_all | solution.py:145
  114.9 0.0 collective-permute-done.7.back
  114.9 7.3 %near.3 = f32[512,128]{1,0:T(8,128)} custom-call(s32[7]{0:T(128)} %select_reduce_fusion.slots, f32[7]{0:T(128)} %bitcast.74, bf16[7,512,512]{2,1,0:T(8,128)(2,1)} %bitcast.67, bf16[512,128]{1,0:T(8,128)(2,1)} %copy-done.1, bf16[512,128]{1,0:T(8,128)(2,1)} %copy-done.11, bf16[2,512,128]{2,1,0:T(8,128)(2,1)} %copy-done.3, bf16[2,512,128]{2,1,0:T(8,128)(2,1)} %copy-done.8, ...), custom_call_target="tpu_custom_call" | custom-call | flops 469762048 | bytes 3670016 | tf_op jit(solution)/shard_map/near/pallas_call | solution.py:66
  122.3 0.0 all-to-all-done.5
  122.3 0.2 convolution_bitcast_fusion
  122.5 1.8 %fusion.16 = (f32[1,512,128]{2,1,0:T(8,128)}, f32[1,512,128]{2,1,0:T(8,128)}) fusion(f32[512,128]{1,0:T(8,128)S(1)} %convolution_bitcast_fusion, f32[512,128]{1,0:T(8,128)S(1)} %copy-done.7, f32[512,128]{1,0:T(8,128)} %near.3, f32[1,512,128]{2,1,0:T(8,128)S(1)} %copy-done.6), kind=kLoop, calls=%fused_computation.45 | loop fusion | flops 327680 | bytes 1572864 | tf_op jit(solution)/shard_map/broadcast_in_dim | solution.py:152
  (24 shorter events, 0.1 us)
Async XLA Ops:
  0.6 64.8 %copy-start = (bf16[1,512,64]{1,2,0:T(8,128)(2,1)S(1)}, bf16[1,512,64]{1,2,0:T(8,128)(2,1)}, u32[]{:S(2)}) copy-start(bf16[1,512,64]{1,2,0:T(8,128)(2,1)} %param.15) | copy-start | bytes 196612
  1.7 35.9 %copy-start.9 = (bf16[512,128]{1,0:T(8,128)(2,1)}, bf16[512,128]{1,0:T(8,128)(2,1)S(1)}, u32[]{:S(2)}) copy-start(bf16[512,128]{1,0:T(8,128)(2,1)S(1)} %get-tuple-element.6.own) | copy-start | bytes 393220
  3.4 16.0 %all-to-all-start = ((bf16[4,64,128]{2,1,0:T(8,128)(2,1)}), bf16[4,64,128]{2,1,0:T(8,128)(2,1)S(1)}, u32[]{:S(2)}, u32[]{:S(2)}) async-start(bf16[4,64,128]{2,1,0:T(8,128)(2,1)} %broadcast_in_dim.38), calls=%async_computation | async-start | bytes 131072 | tf_op jit(solution)/shard_map/all_to_all | solution.py:32
  12.4 15.2 %collective-permute-start = (bf16[512,128]{1,0:T(8,128)(2,1)S(1)}, bf16[512,128]{1,0:T(8,128)(2,1)S(1)}, u32[]{:S(2)}, u32[]{:S(2)}) collective-permute-start(bf16[512,128]{1,0:T(8,128)(2,1)S(1)} %get-tuple-element.6.own), channel_id=1, source_target_pairs={{0,1},{1,0},{2,3},{3,2},{4,5},{5,4},{6,7},{7,6},{8,9},{9,8},{10,11... | collective-permute-start | bytes 393224 | tf_op jit(solution)/shard_map/ppermute | solution.py:19
  20.8 31.3 %all-to-all-start.1 = ((bf16[16,4,64,128]{3,2,1,0:T(8,128)(2,1)}), bf16[16,4,64,128]{3,2,1,0:T(8,128)(2,1)S(1)}, u32[]{:S(2)}, u32[]{:S(2)}) async-start(bf16[16,4,64,128]{3,2,1,0:T(8,128)(2,1)} %broadcast_in_dim.39), calls=%async_computation.1 | async-start | bytes 2097152 | tf_op jit(solution)/shard_map/all_to_all | solution.py:32
  27.7 10.0 %copy-start.10 = (bf16[512,128]{1,0:T(8,128)(2,1)}, bf16[512,128]{1,0:T(8,128)(2,1)S(1)}, u32[]{:S(2)}) copy-start(bf16[512,128]{1,0:T(8,128)(2,1)S(1)} %collective-permute-done.other) | copy-start | bytes 393220
  28.4 22.8 %collective-permute-start.1 = (bf16[2,512,128]{2,1,0:T(8,128)(2,1)}, bf16[2,512,128]{2,1,0:T(8,128)(2,1)S(1)}, u32[]{:S(2)}, u32[]{:S(2)}) collective-permute-start(bf16[2,512,128]{2,1,0:T(8,128)(2,1)} %pad_maximum_fusion.2), channel_id=1, source_target_pairs={{0,2},{1,255},{2,4},{3,1},{4,6},{5,3},{6,8},{7,5},{8,10},{9,7},{10... | collective-permute-start | bytes 786440 | tf_op jit(solution)/shard_map/ppermute | solution.py:19
  32.5 17.8 %collective-permute-start.2 = (bf16[2,512,128]{2,1,0:T(8,128)(2,1)}, bf16[2,512,128]{2,1,0:T(8,128)(2,1)}, u32[]{:S(2)}, u32[]{:S(2)}) collective-permute-start(bf16[2,512,128]{2,1,0:T(8,128)(2,1)} %pad_maximum_fusion.2), channel_id=1, source_target_pairs={{0,4},{1,253},{2,6},{3,255},{4,8},{5,1},{6,10},{7,3},{8,12},{9,5},... | collective-permute-start | bytes 786440 | tf_op jit(solution)/shard_map/ppermute | solution.py:19
  44.6 5.7 %copy-start.13 = (s32[1,7]{1,0:T(1,128)S(1)}, s32[1,7]{1,0:T(1,128)}, u32[]{:S(2)}) copy-start(s32[1,7]{1,0:T(1,128)} %param.13) | copy-start | bytes 88
  50.3 7.0 %copy-start.14 = (s32[9]{0:T(128)S(1)}, s32[9]{0:T(128)}, u32[]{:S(2)}) copy-start(s32[9]{0:T(128)} %constant.69.clone) | copy-start | bytes 112
  51.3 6.8 %copy-start.2 = (bf16[2,512,128]{2,1,0:T(8,128)(2,1)}, bf16[2,512,128]{2,1,0:T(8,128)(2,1)S(1)}, u32[]{:S(2)}) copy-start(bf16[2,512,128]{2,1,0:T(8,128)(2,1)S(1)} %collective-permute-done.1.first) | copy-start | bytes 786436
  52.1 5.9 %collective-permute-start.3 = (bf16[3,512,128]{2,1,0:T(8,128)(2,1)}, bf16[3,512,128]{2,1,0:T(8,128)(2,1)}, u32[]{:S(2)}, u32[]{:S(2)}) collective-permute-start(bf16[3,512,128]{2,1,0:T(8,128)(2,1)} %pad_maximum_fusion), channel_id=1, source_target_pairs={{0,1},{1,0},{2,3},{3,2},{4,5},{5,4},{6,7},{7,6},{8,9},{9,8},{10,11... | collective-permute-start | bytes 1179656 | tf_op jit(solution)/shard_map/ppermute | solution.py:19
  53.4 12.3 %copy-start.4 = (f32[1,512,128]{2,1,0:T(8,128)S(1)}, f32[1,512,128]{2,1,0:T(8,128)}, u32[]{:S(2)}) copy-start(f32[1,512,128]{2,1,0:T(8,128)} %param.10) | copy-start | bytes 786436
  53.4 12.3 %copy-start.5 = (f32[1,512,128]{2,1,0:T(8,128)S(1)}, f32[1,512,128]{2,1,0:T(8,128)}, u32[]{:S(2)}) copy-start(f32[1,512,128]{2,1,0:T(8,128)} %param.9) | copy-start | bytes 786436
  53.4 14.0 %copy-start.12 = (bf16[1,512,64]{1,2,0:T(8,128)(2,1)S(1)}, bf16[1,512,64]{1,2,0:T(8,128)(2,1)}, u32[]{:S(2)}) copy-start(bf16[1,512,64]{1,2,0:T(8,128)(2,1)} %param.14) | copy-start | bytes 196612
  53.4 12.0 %all-to-all-start.2 = ((bf16[4,64,128]{2,1,0:T(8,128)(2,1)}), bf16[4,64,128]{2,1,0:T(8,128)(2,1)S(1)}, u32[]{:S(2)}, u32[]{:S(2)}) async-start(bf16[4,64,128]{2,1,0:T(8,128)(2,1)} %bitcast.10), calls=%async_computation.2 | async-start | bytes 131072 | tf_op jit(solution)/shard_map/all_to_all | solution.py:145
  67.4 43.5 %copy-start.1 = (bf16[512,128]{1,0:T(8,128)(2,1)}, bf16[512,128]{1,0:T(8,128)(2,1)S(1)}, u32[]{:S(2)}) copy-start(bf16[512,128]{1,0:T(8,128)(2,1)S(1)} %get-tuple-element.2.own) | copy-start | bytes 393220
  80.2 29.4 %all-to-all-start.4 = ((bf16[16,4,64,128]{3,2,1,0:T(8,128)(2,1)}), bf16[16,4,64,128]{3,2,1,0:T(8,128)(2,1)S(1)}, u32[]{:S(2)}, u32[]{:S(2)}) async-start(bf16[16,4,64,128]{3,2,1,0:T(8,128)(2,1)} %broadcast_in_dim.41), calls=%async_computation.4 | async-start | bytes 2097152 | tf_op jit(solution)/shard_map/all_to_all | solution.py:32
  86.4 3.3 %collective-permute-start.4 = (bf16[512,128]{1,0:T(8,128)(2,1)S(1)}, bf16[512,128]{1,0:T(8,128)(2,1)S(1)}, u32[]{:S(2)}, u32[]{:S(2)}) collective-permute-start(bf16[512,128]{1,0:T(8,128)(2,1)S(1)} %get-tuple-element.2.own), channel_id=1, source_target_pairs={{0,1},{1,0},{2,3},{3,2},{4,5},{5,4},{6,7},{7,6},{8,9},{9,8},{10,11... | collective-permute-start | bytes 393224 | tf_op jit(solution)/shard_map/ppermute | solution.py:19
  89.7 25.3 %copy-start.11 = (bf16[512,128]{1,0:T(8,128)(2,1)}, bf16[512,128]{1,0:T(8,128)(2,1)S(1)}, u32[]{:S(2)}) copy-start(bf16[512,128]{1,0:T(8,128)(2,1)S(1)} %collective-permute-done.4.other) | copy-start | bytes 393220
  89.7 10.8 %collective-permute-start.6 = (bf16[2,512,128]{2,1,0:T(8,128)(2,1)S(1)}, bf16[2,512,128]{2,1,0:T(8,128)(2,1)S(1)}, u32[]{:S(2)}, u32[]{:S(2)}) collective-permute-start(bf16[2,512,128]{2,1,0:T(8,128)(2,1)S(1)} %pad_maximum_fusion.3), channel_id=1, source_target_pairs={{0,4},{1,253},{2,6},{3,255},{4,8},{5,1},{6,10},{7,3},{8,12},{9,5},... | collective-permute-start | bytes 786440 | tf_op jit(solution)/shard_map/ppermute | solution.py:19
  94.4 9.5 %collective-permute-start.5 = (bf16[2,512,128]{2,1,0:T(8,128)(2,1)S(1)}, bf16[2,512,128]{2,1,0:T(8,128)(2,1)S(1)}, u32[]{:S(2)}, u32[]{:S(2)}) collective-permute-start(bf16[2,512,128]{2,1,0:T(8,128)(2,1)S(1)} %pad_maximum_fusion.3), channel_id=1, source_target_pairs={{0,2},{1,255},{2,4},{3,1},{4,6},{5,3},{6,8},{7,5},{8,10},{9,7},{10... | collective-permute-start | bytes 786440 | tf_op jit(solution)/shard_map/ppermute | solution.py:19
  100.5 0.7 copy-start.8
  103.8 0.8 copy-start.3
  104.7 10.3 %collective-permute-start.7 = (bf16[3,512,128]{2,1,0:T(8,128)(2,1)}, bf16[3,512,128]{2,1,0:T(8,128)(2,1)}, u32[]{:S(2)}, u32[]{:S(2)}) collective-permute-start(bf16[3,512,128]{2,1,0:T(8,128)(2,1)} %pad_maximum_fusion.1), channel_id=1, source_target_pairs={{0,1},{1,0},{2,3},{3,2},{4,5},{5,4},{6,7},{7,6},{8,9},{9,8},{10,11... | collective-permute-start | bytes 1179656 | tf_op jit(solution)/shard_map/ppermute | solution.py:19
  110.9 11.6 %copy-start.6 = (f32[1,512,128]{2,1,0:T(8,128)S(1)}, f32[1,512,128]{2,1,0:T(8,128)}, u32[]{:S(2)}) copy-start(f32[1,512,128]{2,1,0:T(8,128)} %param.9) | copy-start | bytes 786436
  110.9 11.6 %copy-start.7 = (f32[512,128]{1,0:T(8,128)S(1)}, f32[512,128]{1,0:T(8,128)}, u32[]{:S(2)}) copy-start(f32[512,128]{1,0:T(8,128)} %get-tuple-element.3) | copy-start | bytes 786436
  110.9 11.4 %all-to-all-start.5 = ((bf16[4,64,128]{2,1,0:T(8,128)(2,1)}), bf16[4,64,128]{2,1,0:T(8,128)(2,1)S(1)}, u32[]{:S(2)}, u32[]{:S(2)}) async-start(bf16[4,64,128]{2,1,0:T(8,128)(2,1)} %bitcast.17), calls=%async_computation.5 | async-start | bytes 131072 | tf_op jit(solution)/shard_map/all_to_all | solution.py:145

commit v2 on v1

v2 whole, which is shorter than its diff:
```python
import jax
import jax.numpy as jnp
from jax import lax
from jax.experimental import pallas as pl
from jax.experimental.pallas import tpu as pltpu
from jax.sharding import PartitionSpec as P

REACH = 4
ITERS = 2
ALL = ("near", "row", "col")

damping = 0.5

SLOTS = (8, 6, 7, 1, 0, 3, 2, 5, 4)
ROW_STEPS = (0, -1, 1, 2)


def moved(value, target):
    count = lax.axis_size(ALL)
    return lax.ppermute(value, ALL, [(source, target(source) % count) for source in range(count)])


def outward(steps):
    return lambda source: source + steps if source % 2 == 0 else source - steps


def crossed(mask):
    return lambda source: source ^ mask


def along_row(value, steps):
    count = lax.axis_size("row")
    return lax.ppermute(value, "row", [(source, (source + steps) % count) for source in range(count)])


def sent_to_all(array, axis):
    copies = jnp.broadcast_to(array, (lax.axis_size(axis), *array.shape))
    return lax.all_to_all(copies, axis, split_axis=0, concat_axis=0, tiled=True)


SMEM = pltpu.MemorySpace.SMEM
HBM = pltpu.MemorySpace.HBM


def base_body(
    slots, scales, tiles, own, other, first, second, back, right, iterate, out,
    tile_buf, window, right_buf, iterate_buf, tile_sems, sems,
):
    count = tiles.shape[0]
    copies = [
        pltpu.make_async_copy(own, window.at[0], sems.at[0]),
        pltpu.make_async_copy(other, window.at[1], sems.at[1]),
        pltpu.make_async_copy(first, window.at[pl.ds(2, 2)], sems.at[2]),
        pltpu.make_async_copy(second, window.at[pl.ds(4, 2)], sems.at[3]),
        pltpu.make_async_copy(back, window.at[pl.ds(6, 3)], sems.at[4]),
    ]
    tile_copies = [
        pltpu.make_async_copy(tiles.at[k], tile_buf.at[k], tile_sems.at[k]) for k in range(count)
    ]
    vector_copies = [
        pltpu.make_async_copy(right, right_buf, sems.at[5]),
        pltpu.make_async_copy(iterate, iterate_buf, sems.at[6]),
    ]
    for copy in copies + tile_copies + vector_copies:
        copy.start()
    for copy in copies:
        copy.wait()
    for k in range(count):
        tile_copies[k].wait()
        product = scales[k] * jnp.dot(
            tile_buf[k], window[slots[k]], preferred_element_type=jnp.float32
        )
        out[...] = product if k == 0 else out[...] + product
    for copy in vector_copies:
        copy.wait()
    out[...] = right_buf[...] - (iterate_buf[...] + out[...])


def base_residual(slots, scales, tiles, own, other, first, second, back, right, iterate):
    count, rows, inner = tiles.shape
    cols = own.shape[-1]
    hbm = pl.BlockSpec(memory_space=HBM)
    smem = pl.BlockSpec(memory_space=SMEM)
    return pl.pallas_call(
        base_body,
        out_shape=jax.ShapeDtypeStruct((rows, cols), jnp.float32),
        in_specs=[smem, smem] + [hbm] * 8,
        out_specs=pl.BlockSpec(memory_space=pltpu.MemorySpace.VMEM),
        scratch_shapes=[
            pltpu.VMEM((count, rows, inner), tiles.dtype),
            pltpu.VMEM((2 * REACH + 1, rows, cols), own.dtype),
            pltpu.VMEM((rows, cols), jnp.float32),
            pltpu.VMEM((rows, cols), jnp.float32),
            pltpu.SemaphoreType.DMA((count,)),
            pltpu.SemaphoreType.DMA((7,)),
        ],
        cost_estimate=pl.CostEstimate(
            flops=2 * count * rows * inner * cols,
            bytes_accessed=2 * count * rows * inner,
            transcendentals=0,
        ),
        name="near",
    )(slots, scales, tiles, own, other, first, second, back, right, iterate)


def layout_body(place, couplings, out, *, clusters, rows):
    group, row, col = place[0], place[1], place[2]
    targets, block, rank, _ = couplings.shape
    step = pl.program_id(0)
    for part in range(block // rows):
        for m in range(targets):
            local = col ^ m
            target = group * targets + local
            pieces = []
            for distance in ROW_STEPS:
                within = part * rows + (row + distance + rows) % rows
                source = (step * block + within) * targets + col
                gap = (target - source + clusters) % clusters
                far = jnp.minimum(gap, clusters - gap) > REACH
                piece = couplings[local, within]
                pieces.append(jnp.where(far, piece, jnp.zeros_like(piece)))
            out[m * rank : (m + 1) * rank, part * rows * rank : (part + 1) * rows * rank] = (
                jnp.concatenate(pieces, axis=1)
            )


def laid_out_couplings(place, couplings, clusters, rows):
    targets, sources, rank, _ = couplings.shape
    block = 4 * rows
    return pl.pallas_call(
        lambda *refs: layout_body(*refs, clusters=clusters, rows=rows),
        out_shape=jax.ShapeDtypeStruct((targets * rank, sources * rank), couplings.dtype),
        grid=(sources // block,),
        in_specs=[
            pl.BlockSpec(memory_space=SMEM),
            pl.BlockSpec((targets, block, rank, rank), lambda k: (0, k, 0, 0)),
        ],
        out_specs=pl.BlockSpec((targets * rank, block * rank), lambda k: (0, k)),
        cost_estimate=pl.CostEstimate(
            flops=0, bytes_accessed=6 * targets * sources * rank * rank, transcendentals=0
        ),
        name="layout",
    )(place, couplings)


def halo(own):
    other = moved(own, crossed(1))
    pair = jnp.stack([own, other])
    first = moved(pair, outward(2))
    second = moved(pair, outward(4))
    back = moved(jnp.concatenate([first, second[1:]]), crossed(1))
    return own, other, first, second, back


def shards(
    right_side,
    start_guess,
    near_tiles,
    tile_scales,
    neighbours,
    source_cluster_basis,
    basis_out,
    couplings,
):
    right_side, iterate = right_side[0], start_guess[0]
    near_tiles, scales = near_tiles[0], tile_scales[0]
    basis_in, basis_out = source_cluster_basis[0], basis_out[0]
    clusters = lax.axis_size(ALL)
    row_count = lax.axis_size("row")
    device = lax.axis_index(ALL)
    side = 2 * (device % 2) - 1
    offsets = jnp.mod(neighbours[0] - device + REACH, clusters) - REACH
    places = jnp.arange(2 * REACH + 1, dtype=jnp.int32)
    chosen = (side * offsets + REACH)[:, None] == places[None, :]
    slots = jnp.sum(jnp.where(chosen, jnp.array(SLOTS, jnp.int32)[None, :], 0), axis=1)

    targets, sources, rank, _ = couplings.shape
    place = jnp.stack([lax.axis_index(("near", "row")), lax.axis_index("row"), lax.axis_index("col")])
    far_rows = laid_out_couplings(place.astype(jnp.int32), couplings, clusters, row_count)

    residual = right_side
    for sweep in range(ITERS):
        coarse = iterate.astype(jnp.bfloat16)
        coefs = jnp.einsum(
            "lr,lc->rc", basis_in, coarse, preferred_element_type=jnp.float32
        ).astype(jnp.bfloat16)
        in_row = jnp.stack(
            [along_row(coefs, -steps) if steps else coefs for steps in ROW_STEPS]
        )
        gathered = sent_to_all(in_row, "near")
        base = base_residual(slots, scales, near_tiles, *halo(coarse), right_side, iterate)
        partial_coefs = (
            jnp.dot(
                far_rows, gathered.reshape(sources * rank, -1), preferred_element_type=jnp.float32
            )
            .astype(jnp.bfloat16)
            .reshape(targets, rank, -1)
        )
        far_coefs = partial_coefs[0].astype(jnp.float32)
        for m in range(1, targets):
            far_coefs += moved(partial_coefs[m], crossed(m)).astype(jnp.float32)
        far_term = jnp.dot(
            basis_out, far_coefs.astype(jnp.bfloat16), preferred_element_type=jnp.float32
        )
        residual = base - far_term
        iterate = iterate + damping * residual
    return (iterate[None], residual[None])


def solution(mesh):
    in_specs = (
        P(ALL, None, None),
        P(ALL, None, None),
        P(ALL, None, None, None),
        P(ALL, None),
        P(ALL, None),
        P(ALL, None, None),
        P(ALL, None, None),
        P(("near", "row"), "col", None, None),
    )
    out_specs = (P(ALL, None, None), P(ALL, None, None))
    return jax.shard_map(shards, mesh=mesh, in_specs=in_specs, out_specs=out_specs, check_vma=False)
```

time: 125 us -> 115 us (0.920)
  local copies, waits for them, and re-layouts: 17.5 us -> 4.07 us
  blocking collectives: 11.3 us -> 0 us
  starting transfers between devices: 47.9 us -> 57 us
  waiting for transfers between devices: 15.4 us -> 23.1 us
  other arithmetic: 12.4 us -> 6.89 us
  Pallas kernels: 14.7 us -> 17.8 us
    ppermute x0 -> x6, starting transfers between devices: none -> 15.5 us  [along_row(): lax.ppermute(value, 'row', [(source, (source + steps) % count) for source...]
    ppermute x8 -> x14, starting transfers between devices: 18.1 us -> 31 us  [moved(): lax.ppermute(value, ALL, [(source, target(source) % count) for source in...]
    all_to_all x3 -> x2, starting transfers between devices: 21.9 us -> 10.5 us  [sent_to_all(): return lax.all_to_all(copies, axis, split_axis=0, concat_axis=0, tiled=True)]
    all_to_all x1 -> x0, blocking collectives: 11.3 us -> none  [sent_to_all(): return lax.all_to_all(copies, axis, split_axis=0, concat_axis=0, tiled=True)]
    ppermute x0 -> x6, waiting for transfers between devices: none -> 8.15 us  [along_row(): lax.ppermute(value, 'row', [(source, (source + steps) % count) for source...]
    all_to_all x2 -> x0, starting transfers between devices: 7.89 us -> none  [shards(): lax.all_to_all(partial_coefs.reshape(targets, rank, -1), 'col', 0, 0, til...]
    transpose x1 -> x0, local copies, waits for them, and re-layouts: 6.91 us -> none  [shards(): jnp.transpose(masked, (0, 2, 1, 3)).reshape(targets * rank, sources * rank)]
    all_to_all x3 -> x2, waiting for transfers between devices: 6.08 us -> 0.01 us  [sent_to_all(): return lax.all_to_all(copies, axis, split_axis=0, concat_axis=0, tiled=True)]
  transfers between devices with their start and end apart: 13 -> 22, of which waited for: 4 -> 8; matrix products, arithmetic and copies ran while one was open for 20% -> 5% of each run, Pallas kernels for 12% -> 16%
where the time goes in v2:
time: 115 us; the launch traced here: 114 us
  starting transfers between devices  57 us (50%)
  waiting for transfers between devices  23.1 us (20%)
  Pallas kernels  17.8 us (15%)
  other arithmetic  6.89 us (6%)
  matrix products  4.63 us (4%)
  local copies, waits for them, and re-layouts  4.07 us (4%)
    ppermute x14, starting transfers between devices, moved(): lax.ppermute(value, ALL, [(source, target(source) % count) for source in...  31 us
    ppermute x6, starting transfers between devices, along_row(): lax.ppermute(value, 'row', [(source, (source + steps) % count) for source...  15.5 us
    ppermute x14, waiting for transfers between devices, moved(): lax.ppermute(value, ALL, [(source, target(source) % count) for source in...  14.9 us
    pallas_call x2, Pallas kernels, base_residual(): pl.pallas_call(base_body, out_shape=jax.ShapeDtypeStruct((rows, cols), jn...  12.8 us
    all_to_all x2, starting transfers between devices, sent_to_all(): return lax.all_to_all(copies, axis, split_axis=0, concat_axis=0, tiled=True)  10.5 us
    ppermute x6, waiting for transfers between devices, along_row(): lax.ppermute(value, 'row', [(source, (source + steps) % count) for source...  8.15 us
    pallas_call x1, Pallas kernels, laid_out_couplings(): pl.pallas_call(lambda *refs: layout_body(*refs, clusters=clusters, rows=r...  4.97 us
    dot_general x2, matrix products, shards(): jnp.dot(far_rows, gathered.reshape(sources * rank, -1), preferred_element...  2.98 us
  transfers between devices with their start and end apart: 22, of which 8 were waited for; matrix products, arithmetic and copies ran while one was open for 5% of the time, Pallas kernels for 16%

profile of v2, /device:TPU:1, one launch (start us, length us, event | category | flops | bytes accessed | tf_op | source)
XLA Modules:
  0.0 114.4 jit_solution(15198321716800207179)
XLA Ops:
  0.6 0.0 copy-start
  0.6 1.1 fusion.12
  1.8 1.0 convolution_convert_fusion.3
  2.8 3.9 %collective-permute-start.4 = (bf16[64,128]{1,0:T(8,128)(2,1)S(1)}, bf16[64,128]{1,0:T(8,128)(2,1)S(1)}, u32[]{:S(2)}, u32[]{:S(2)}) collective-permute-start(bf16[64,128]{1,0:T(8,128)(2,1)S(1)} %convolution_convert_fusion.3), channel_id=1, source_target_pairs={{0,4},{4,8},{8,12},{12,0},{1,5},{5,9},{9,13},{13,1},{2,6},{6,10},{... | collective-permute-start | bytes 49160 | tf_op jit(solution)/shard_map/ppermute | solution.py:33
  6.7 3.1 %collective-permute-start.5 = (bf16[64,128]{1,0:T(8,128)(2,1)S(1)}, bf16[64,128]{1,0:T(8,128)(2,1)S(1)}, u32[]{:S(2)}, u32[]{:S(2)}) collective-permute-start(bf16[64,128]{1,0:T(8,128)(2,1)S(1)} %convolution_convert_fusion.3), channel_id=1, source_target_pairs={{0,12},{4,0},{8,4},{12,8},{1,13},{5,1},{9,5},{13,9},{2,14},{6,2},{... | collective-permute-start | bytes 49160 | tf_op jit(solution)/shard_map/ppermute | solution.py:33
  9.8 4.4 %collective-permute-start.6 = (bf16[64,128]{1,0:T(8,128)(2,1)S(1)}, bf16[64,128]{1,0:T(8,128)(2,1)S(1)}, u32[]{:S(2)}, u32[]{:S(2)}) collective-permute-start(bf16[64,128]{1,0:T(8,128)(2,1)S(1)} %convolution_convert_fusion.3), channel_id=1, source_target_pairs={{0,8},{4,12},{8,0},{12,4},{1,9},{5,13},{9,1},{13,5},{2,10},{6,14},... | collective-permute-start | bytes 49160 | tf_op jit(solution)/shard_map/ppermute | solution.py:33
  14.2 0.0 collective-permute-done.4
  14.2 0.0 collective-permute-done.5
  14.2 2.1 %collective-permute-done.6 = bf16[64,128]{1,0:T(8,128)(2,1)S(1)} collective-permute-done((bf16[64,128]{1,0:T(8,128)(2,1)S(1)}, bf16[64,128]{1,0:T(8,128)(2,1)S(1)}, u32[]{:S(2)}, u32[]{:S(2)}) %collective-permute-start.6) | collective-permute-done | bytes 16416 | tf_op jit(solution)/shard_map/ppermute | solution.py:33
  16.3 1.3 %broadcast_in_dim.29 = bf16[16,4,64,128]{3,2,1,0:T(8,128)(2,1)} broadcast(bf16[4,64,128]{2,1,0:T(8,128)(2,1)S(1)} %pad_maximum_fusion.4), dimensions={1,2,3} | broadcast | bytes 1114112 | tf_op jit(solution)/shard_map/broadcast_in_dim | solution.py:37
  17.6 6.8 %all-to-all-start = ((bf16[16,4,64,128]{3,2,1,0:T(8,128)(2,1)}), bf16[16,4,64,128]{3,2,1,0:T(8,128)(2,1)S(1)}, u32[]{:S(2)}, u32[]{:S(2)}) async-start(bf16[16,4,64,128]{3,2,1,0:T(8,128)(2,1)} %broadcast_in_dim.29), calls=%async_computation | async-start | bytes 2097152 | tf_op jit(solution)/shard_map/all_to_all | solution.py:38
  24.3 2.5 %collective-permute-start = (bf16[512,128]{1,0:T(8,128)(2,1)S(1)}, bf16[512,128]{1,0:T(8,128)(2,1)S(1)}, u32[]{:S(2)}, u32[]{:S(2)}) collective-permute-start(bf16[512,128]{1,0:T(8,128)(2,1)S(1)} %get-tuple-element.7.own), channel_id=1, source_target_pairs={{0,1},{1,0},{2,3},{3,2},{4,5},{5,4},{6,7},{7,6},{8,9},{9,8},{10,11... | collective-permute-start | bytes 393224 | tf_op jit(solution)/shard_map/ppermute | solution.py:20
  26.8 0.6 pad_add_fusion.refs_0_
  27.4 5.0 %layout.1 = bf16[256,4096]{1,0:T(8,128)(2,1)} custom-call(s32[3]{0:T(128)} %pad_add_fusion.refs_0_, bf16[4,64,64,64]{3,2,1,0:T(8,128)(2,1)} %refs_1_.1), custom_call_target="tpu_custom_call" | custom-call | bytes 6291456 | tf_op jit(solution)/shard_map/layout/pallas_call | solution.py:130
  32.4 0.0 collective-permute-done.other
  32.4 7.2 %collective-permute-start.2 = (bf16[2,512,128]{2,1,0:T(8,128)(2,1)S(1)}, bf16[2,512,128]{2,1,0:T(8,128)(2,1)S(1)}, u32[]{:S(2)}, u32[]{:S(2)}) collective-permute-start(bf16[2,512,128]{2,1,0:T(8,128)(2,1)S(1)} %pad_maximum_fusion.2), channel_id=1, source_target_pairs={{0,4},{1,253},{2,6},{3,255},{4,8},{5,1},{6,10},{7,3},{8,12},{9,5},... | collective-permute-start | bytes 786440 | tf_op jit(solution)/shard_map/ppermute | solution.py:20
  39.7 1.9 %collective-permute-start.1 = (bf16[2,512,128]{2,1,0:T(8,128)(2,1)S(1)}, bf16[2,512,128]{2,1,0:T(8,128)(2,1)S(1)}, u32[]{:S(2)}, u32[]{:S(2)}) collective-permute-start(bf16[2,512,128]{2,1,0:T(8,128)(2,1)S(1)} %pad_maximum_fusion.2), channel_id=1, source_target_pairs={{0,2},{1,255},{2,4},{3,1},{4,6},{5,3},{6,8},{7,5},{8,10},{9,7},{10... | collective-permute-start | bytes 786440 | tf_op jit(solution)/shard_map/ppermute | solution.py:20
  41.6 0.7 select_reduce_fusion.slots
  42.4 3.4 %collective-permute-done.2.second = bf16[2,512,128]{2,1,0:T(8,128)(2,1)S(1)} collective-permute-done((bf16[2,512,128]{2,1,0:T(8,128)(2,1)S(1)}, bf16[2,512,128]{2,1,0:T(8,128)(2,1)S(1)}, u32[]{:S(2)}, u32[]{:S(2)}) %collective-permute-start.2) | collective-permute-done | bytes 262176 | tf_op jit(solution)/shard_map/ppermute | solution.py:20
  45.8 2.8 %collective-permute-done.1.first = bf16[2,512,128]{2,1,0:T(8,128)(2,1)S(1)} collective-permute-done((bf16[2,512,128]{2,1,0:T(8,128)(2,1)S(1)}, bf16[2,512,128]{2,1,0:T(8,128)(2,1)S(1)}, u32[]{:S(2)}, u32[]{:S(2)}) %collective-permute-start.1) | collective-permute-done | bytes 262176 | tf_op jit(solution)/shard_map/ppermute | solution.py:20
  48.7 1.9 %collective-permute-start.3 = (bf16[3,512,128]{2,1,0:T(8,128)(2,1)S(1)}, bf16[3,512,128]{2,1,0:T(8,128)(2,1)S(1)}, u32[]{:S(2)}, u32[]{:S(2)}) collective-permute-start(bf16[3,512,128]{2,1,0:T(8,128)(2,1)S(1)} %pad_maximum_fusion), channel_id=1, source_target_pairs={{0,1},{1,0},{2,3},{3,2},{4,5},{5,4},{6,7},{7,6},{8,9},{9,8},{10,11... | collective-permute-start | bytes 1179656 | tf_op jit(solution)/shard_map/ppermute | solution.py:20
  50.6 0.0 all-to-all-done
  50.6 2.3 %convolution_convert_fusion.1 = bf16[256,128]{1,0:T(8,128)(2,1)S(1)} fusion(bf16[256,4096]{1,0:T(8,128)(2,1)} %layout.1, bf16[4096,128]{1,0:T(8,128)(2,1)S(1)} %bitcast.55), kind=kOutput, calls=%fused_computation.3 | convolution fusion | flops 268468224 | bytes 3211264 | tf_op jit(solution)/shard_map/dot_general | solution.py:193
  52.9 0.1 collective-permute-start.7
  53.0 0.1 collective-permute-start.8
  53.1 2.0 %collective-permute-start.9 = (bf16[64,128]{1,0:T(8,128)(2,1)S(1)}, bf16[64,128]{1,0:T(8,128)(2,1)S(1)}, u32[]{:S(2)}, u32[]{:S(2)}) collective-permute-start(bf16[64,128]{1,0:T(8,128)(2,1)S(1)} %get-tuple-element.12), channel_id=1, source_target_pairs={{0,3},{1,2},{2,1},{3,0},{4,7},{5,6},{6,5},{7,4},{8,11},{9,10},{10,... | collective-permute-start | bytes 49160 | tf_op jit(solution)/shard_map/ppermute | solution.py:20
  55.1 0.0 collective-permute-done.3.back
  55.1 0.8 copy-done.12
  55.9 6.4 %near.2 = f32[512,128]{1,0:T(8,128)} custom-call(s32[7]{0:T(128)} %select_reduce_fusion.slots, f32[7]{0:T(128)} %bitcast.74, bf16[7,512,512]{2,1,0:T(8,128)(2,1)} %bitcast.53, bf16[512,128]{1,0:T(8,128)(2,1)} %copy-done.9, bf16[512,128]{1,0:T(8,128)(2,1)} %copy-done.10, bf16[2,512,128]{2,1,0:T(8,128)(2,1)} %copy-done.5, bf16[2,512,128]{2,1,0:T(8,128)(2,1)} %copy-done.7, ...), custom_call_target="tpu_custom_call" | custom-call | flops 469762048 | bytes 3670016 | tf_op jit(solution)/shard_map/near/pallas_call | solution.py:84
  62.3 0.0 collective-permute-done.7
  62.3 0.0 collective-permute-done.8
  62.3 0.0 collective-permute-done.9
  62.3 0.2 convolution_bitcast_fusion.1
  62.6 1.7 %fusion.11 = (bf16[512,128]{1,0:T(8,128)(2,1)S(1)}, f32[512,128]{1,0:T(8,128)}) fusion(f32[512,128]{1,0:T(8,128)} %near.2, f32[512,128]{1,0:T(8,128)S(1)} %convolution_bitcast_fusion.1, f32[1,512,128]{2,1,0:T(8,128)S(1)} %copy-done.3), kind=kLoop, calls=%fused_computation.35 | loop fusion | flops 262144 | bytes 1179648 | tf_op jit(solution)/shard_map/convert_element_type | solution.py:183
  64.3 0.2 convolution_convert_fusion.2
  64.5 0.1 collective-permute-start.14
  64.5 3.6 %collective-permute-start.15 = (bf16[64,128]{1,0:T(8,128)(2,1)S(1)}, bf16[64,128]{1,0:T(8,128)(2,1)S(1)}, u32[]{:S(2)}, u32[]{:S(2)}) collective-permute-start(bf16[64,128]{1,0:T(8,128)(2,1)S(1)} %bitcast.65), channel_id=1, source_target_pairs={{0,12},{4,0},{8,4},{12,8},{1,13},{5,1},{9,5},{13,9},{2,14},{6,2},{... | collective-permute-start | bytes 49160 | tf_op jit(solution)/shard_map/ppermute | solution.py:33
  68.1 0.5 collective-permute-start.16
  68.6 0.7 collective-permute-done.14
  69.2 0.0 collective-permute-done.15
  69.2 5.4 %collective-permute-done.16 = bf16[64,128]{1,0:T(8,128)(2,1)S(1)} collective-permute-done((bf16[64,128]{1,0:T(8,128)(2,1)S(1)}, bf16[64,128]{1,0:T(8,128)(2,1)S(1)}, u32[]{:S(2)}, u32[]{:S(2)}) %collective-permute-start.16) | collective-permute-done | bytes 16416 | tf_op jit(solution)/shard_map/ppermute | solution.py:33
  74.6 1.3 %broadcast_in_dim.30 = bf16[16,4,64,128]{3,2,1,0:T(8,128)(2,1)} broadcast(bf16[4,64,128]{2,1,0:T(8,128)(2,1)S(1)} %pad_maximum_fusion.5), dimensions={1,2,3} | broadcast | bytes 1114112 | tf_op jit(solution)/shard_map/broadcast_in_dim | solution.py:37
  75.9 3.8 %all-to-all-start.1 = ((bf16[16,4,64,128]{3,2,1,0:T(8,128)(2,1)}), bf16[16,4,64,128]{3,2,1,0:T(8,128)(2,1)S(1)}, u32[]{:S(2)}, u32[]{:S(2)}) async-start(bf16[16,4,64,128]{3,2,1,0:T(8,128)(2,1)} %broadcast_in_dim.30), calls=%async_computation.1 | async-start | bytes 2097152 | tf_op jit(solution)/shard_map/all_to_all | solution.py:38
  79.7 1.9 %collective-permute-start.10 = (bf16[512,128]{1,0:T(8,128)(2,1)S(1)}, bf16[512,128]{1,0:T(8,128)(2,1)S(1)}, u32[]{:S(2)}, u32[]{:S(2)}) collective-permute-start(bf16[512,128]{1,0:T(8,128)(2,1)S(1)} %get-tuple-element.2.own), channel_id=1, source_target_pairs={{0,1},{1,0},{2,3},{3,2},{4,5},{5,4},{6,7},{7,6},{8,9},{9,8},{10,11... | collective-permute-start | bytes 393224 | tf_op jit(solution)/shard_map/ppermute | solution.py:20
  81.6 1.0 collective-permute-done.10.other
  82.6 7.1 %collective-permute-start.12 = (bf16[2,512,128]{2,1,0:T(8,128)(2,1)S(1)}, bf16[2,512,128]{2,1,0:T(8,128)(2,1)S(1)}, u32[]{:S(2)}, u32[]{:S(2)}) collective-permute-start(bf16[2,512,128]{2,1,0:T(8,128)(2,1)S(1)} %pad_maximum_fusion.3), channel_id=1, source_target_pairs={{0,4},{1,253},{2,6},{3,255},{4,8},{5,1},{6,10},{7,3},{8,12},{9,5},... | collective-permute-start | bytes 786440 | tf_op jit(solution)/shard_map/ppermute | solution.py:20
  89.7 0.6 collective-permute-start.11
  90.3 5.5 %collective-permute-done.12.second = bf16[2,512,128]{2,1,0:T(8,128)(2,1)S(1)} collective-permute-done((bf16[2,512,128]{2,1,0:T(8,128)(2,1)S(1)}, bf16[2,512,128]{2,1,0:T(8,128)(2,1)S(1)}, u32[]{:S(2)}, u32[]{:S(2)}) %collective-permute-start.12) | collective-permute-done | bytes 262176 | tf_op jit(solution)/shard_map/ppermute | solution.py:20
  95.8 0.7 copy-done.8
  96.6 2.1 %collective-permute-done.11.first = bf16[2,512,128]{2,1,0:T(8,128)(2,1)S(1)} collective-permute-done((bf16[2,512,128]{2,1,0:T(8,128)(2,1)S(1)}, bf16[2,512,128]{2,1,0:T(8,128)(2,1)S(1)}, u32[]{:S(2)}, u32[]{:S(2)}) %collective-permute-start.11) | collective-permute-done | bytes 262176 | tf_op jit(solution)/shard_map/ppermute | solution.py:20
  98.7 0.8 pad_maximum_fusion.1
  99.5 2.8 %collective-permute-start.13 = (bf16[3,512,128]{2,1,0:T(8,128)(2,1)}, bf16[3,512,128]{2,1,0:T(8,128)(2,1)}, u32[]{:S(2)}, u32[]{:S(2)}) collective-permute-start(bf16[3,512,128]{2,1,0:T(8,128)(2,1)} %pad_maximum_fusion.1), channel_id=1, source_target_pairs={{0,1},{1,0},{2,3},{3,2},{4,5},{5,4},{6,7},{7,6},{8,9},{9,8},{10,11... | collective-permute-start | bytes 1179656 | tf_op jit(solution)/shard_map/ppermute | solution.py:20
  102.3 0.0 all-to-all-done.1
  102.3 0.7 convolution_convert_fusion
  103.1 1.1 collective-permute-start.17
  104.2 0.0 collective-permute-start.18
  104.2 1.7 %collective-permute-start.19 = (bf16[64,128]{1,0:T(8,128)(2,1)S(1)}, bf16[64,128]{1,0:T(8,128)(2,1)S(1)}, u32[]{:S(2)}, u32[]{:S(2)}) collective-permute-start(bf16[64,128]{1,0:T(8,128)(2,1)S(1)} %get-tuple-element.9), channel_id=1, source_target_pairs={{0,3},{1,2},{2,1},{3,0},{4,7},{5,6},{6,5},{7,4},{8,11},{9,10},{10,... | collective-permute-start | bytes 49160 | tf_op jit(solution)/shard_map/ppermute | solution.py:20
  105.9 0.0 collective-permute-done.13.back
  105.9 6.4 %near.3 = f32[512,128]{1,0:T(8,128)} custom-call(s32[7]{0:T(128)} %select_reduce_fusion.slots, f32[7]{0:T(128)} %bitcast.75, bf16[7,512,512]{2,1,0:T(8,128)(2,1)} %bitcast.54, bf16[512,128]{1,0:T(8,128)(2,1)} %copy-done.4, bf16[512,128]{1,0:T(8,128)(2,1)} %copy-done.11, bf16[2,512,128]{2,1,0:T(8,128)(2,1)} %copy-done.6, bf16[2,512,128]{2,1,0:T(8,128)(2,1)} %copy-done.8, ...), custom_call_target="tpu_custom_call" | custom-call | flops 469762048 | bytes 3670016 | tf_op jit(solution)/shard_map/near/pallas_call | solution.py:84
  112.3 0.0 collective-permute-done.17
  112.3 0.0 collective-permute-done.18
  112.3 0.0 collective-permute-done.19
  112.4 0.2 convolution_bitcast_fusion
  112.6 1.8 %subtract_bitcast_fusion = (f32[1,512,128]{2,1,0:T(8,128)}, f32[1,512,128]{2,1,0:T(8,128)}) fusion(f32[512,128]{1,0:T(8,128)} %near.3, f32[512,128]{1,0:T(8,128)S(1)} %convolution_bitcast_fusion, f32[512,128]{1,0:T(8,128)S(1)} %copy-done.2), kind=kLoop, calls=%fused_computation.13 | loop fusion | flops 196608 | bytes 1310720 | tf_op jit(solution)/shard_map/broadcast_in_dim | solution.py:207
  (39 shorter events, 0.2 us)
Async XLA Ops:
  0.6 61.7 %copy-start = (bf16[1,512,64]{1,2,0:T(8,128)(2,1)S(1)}, bf16[1,512,64]{1,2,0:T(8,128)(2,1)}, u32[]{:S(2)}) copy-start(bf16[1,512,64]{1,2,0:T(8,128)(2,1)} %param.15) | copy-start | bytes 196612
  1.7 30.7 %copy-start.9 = (bf16[512,128]{1,0:T(8,128)(2,1)}, bf16[512,128]{1,0:T(8,128)(2,1)S(1)}, u32[]{:S(2)}) copy-start(bf16[512,128]{1,0:T(8,128)(2,1)S(1)} %get-tuple-element.7.own) | copy-start | bytes 393220
  2.8 11.4 %collective-permute-start.4 = (bf16[64,128]{1,0:T(8,128)(2,1)S(1)}, bf16[64,128]{1,0:T(8,128)(2,1)S(1)}, u32[]{:S(2)}, u32[]{:S(2)}) collective-permute-start(bf16[64,128]{1,0:T(8,128)(2,1)S(1)} %convolution_convert_fusion.3), channel_id=1, source_target_pairs={{0,4},{4,8},{8,12},{12,0},{1,5},{5,9},{9,13},{13,1},{2,6},{6,10},{... | collective-permute-start | bytes 49160 | tf_op jit(solution)/shard_map/ppermute | solution.py:33
  6.7 7.5 %collective-permute-start.5 = (bf16[64,128]{1,0:T(8,128)(2,1)S(1)}, bf16[64,128]{1,0:T(8,128)(2,1)S(1)}, u32[]{:S(2)}, u32[]{:S(2)}) collective-permute-start(bf16[64,128]{1,0:T(8,128)(2,1)S(1)} %convolution_convert_fusion.3), channel_id=1, source_target_pairs={{0,12},{4,0},{8,4},{12,8},{1,13},{5,1},{9,5},{13,9},{2,14},{6,2},{... | collective-permute-start | bytes 49160 | tf_op jit(solution)/shard_map/ppermute | solution.py:33
  9.8 6.5 %collective-permute-start.6 = (bf16[64,128]{1,0:T(8,128)(2,1)S(1)}, bf16[64,128]{1,0:T(8,128)(2,1)S(1)}, u32[]{:S(2)}, u32[]{:S(2)}) collective-permute-start(bf16[64,128]{1,0:T(8,128)(2,1)S(1)} %convolution_convert_fusion.3), channel_id=1, source_target_pairs={{0,8},{4,12},{8,0},{12,4},{1,9},{5,13},{9,1},{13,5},{2,10},{6,14},... | collective-permute-start | bytes 49160 | tf_op jit(solution)/shard_map/ppermute | solution.py:33
  17.6 33.0 %all-to-all-start = ((bf16[16,4,64,128]{3,2,1,0:T(8,128)(2,1)}), bf16[16,4,64,128]{3,2,1,0:T(8,128)(2,1)S(1)}, u32[]{:S(2)}, u32[]{:S(2)}) async-start(bf16[16,4,64,128]{3,2,1,0:T(8,128)(2,1)} %broadcast_in_dim.29), calls=%async_computation | async-start | bytes 2097152 | tf_op jit(solution)/shard_map/all_to_all | solution.py:38
  24.3 8.1 %collective-permute-start = (bf16[512,128]{1,0:T(8,128)(2,1)S(1)}, bf16[512,128]{1,0:T(8,128)(2,1)S(1)}, u32[]{:S(2)}, u32[]{:S(2)}) collective-permute-start(bf16[512,128]{1,0:T(8,128)(2,1)S(1)} %get-tuple-element.7.own), channel_id=1, source_target_pairs={{0,1},{1,0},{2,3},{3,2},{4,5},{5,4},{6,7},{7,6},{8,9},{9,8},{10,11... | collective-permute-start | bytes 393224 | tf_op jit(solution)/shard_map/ppermute | solution.py:20
  27.4 14.2 %copy-start.14 = (s32[1,7]{1,0:T(1,128)S(1)}, s32[1,7]{1,0:T(1,128)}, u32[]{:S(2)}) copy-start(s32[1,7]{1,0:T(1,128)} %param.13) | copy-start | bytes 88
  27.4 14.2 %copy-start.15 = (s32[9]{0:T(128)S(1)}, s32[9]{0:T(128)}, u32[]{:S(2)}) copy-start(s32[9]{0:T(128)} %constant.54.clone) | copy-start | bytes 112
  32.4 20.4 %copy-start.10 = (bf16[512,128]{1,0:T(8,128)(2,1)}, bf16[512,128]{1,0:T(8,128)(2,1)S(1)}, u32[]{:S(2)}) copy-start(bf16[512,128]{1,0:T(8,128)(2,1)S(1)} %collective-permute-done.other) | copy-start | bytes 393220
  32.4 13.4 %collective-permute-start.2 = (bf16[2,512,128]{2,1,0:T(8,128)(2,1)S(1)}, bf16[2,512,128]{2,1,0:T(8,128)(2,1)S(1)}, u32[]{:S(2)}, u32[]{:S(2)}) collective-permute-start(bf16[2,512,128]{2,1,0:T(8,128)(2,1)S(1)} %pad_maximum_fusion.2), channel_id=1, source_target_pairs={{0,4},{1,253},{2,6},{3,255},{4,8},{5,1},{6,10},{7,3},{8,12},{9,5},... | collective-permute-start | bytes 786440 | tf_op jit(solution)/shard_map/ppermute | solution.py:20
  39.7 8.9 %collective-permute-start.1 = (bf16[2,512,128]{2,1,0:T(8,128)(2,1)S(1)}, bf16[2,512,128]{2,1,0:T(8,128)(2,1)S(1)}, u32[]{:S(2)}, u32[]{:S(2)}) collective-permute-start(bf16[2,512,128]{2,1,0:T(8,128)(2,1)S(1)} %pad_maximum_fusion.2), channel_id=1, source_target_pairs={{0,2},{1,255},{2,4},{3,1},{4,6},{5,3},{6,8},{7,5},{8,10},{9,7},{10... | collective-permute-start | bytes 786440 | tf_op jit(solution)/shard_map/ppermute | solution.py:20
  45.8 7.1 %copy-start.7 = (bf16[2,512,128]{2,1,0:T(8,128)(2,1)}, bf16[2,512,128]{2,1,0:T(8,128)(2,1)S(1)}, u32[]{:S(2)}) copy-start(bf16[2,512,128]{2,1,0:T(8,128)(2,1)S(1)} %collective-permute-done.2.second) | copy-start | bytes 786436
  48.6 6.5 %copy-start.5 = (bf16[2,512,128]{2,1,0:T(8,128)(2,1)}, bf16[2,512,128]{2,1,0:T(8,128)(2,1)S(1)}, u32[]{:S(2)}) copy-start(bf16[2,512,128]{2,1,0:T(8,128)(2,1)S(1)} %collective-permute-done.1.first) | copy-start | bytes 786436
  48.7 6.5 %collective-permute-start.3 = (bf16[3,512,128]{2,1,0:T(8,128)(2,1)S(1)}, bf16[3,512,128]{2,1,0:T(8,128)(2,1)S(1)}, u32[]{:S(2)}, u32[]{:S(2)}) collective-permute-start(bf16[3,512,128]{2,1,0:T(8,128)(2,1)S(1)} %pad_maximum_fusion), channel_id=1, source_target_pairs={{0,1},{1,0},{2,3},{3,2},{4,5},{5,4},{6,7},{7,6},{8,9},{9,8},{10,11... | collective-permute-start | bytes 1179656 | tf_op jit(solution)/shard_map/ppermute | solution.py:20
  52.9 9.4 %collective-permute-start.7 = (bf16[64,128]{1,0:T(8,128)(2,1)S(1)}, bf16[64,128]{1,0:T(8,128)(2,1)S(1)}, u32[]{:S(2)}, u32[]{:S(2)}) collective-permute-start(bf16[64,128]{1,0:T(8,128)(2,1)S(1)} %get-tuple-element.11), channel_id=1, source_target_pairs={{0,1},{1,0},{2,3},{3,2},{4,5},{5,4},{6,7},{7,6},{8,9},{9,8},{10,11... | collective-permute-start | bytes 49160 | tf_op jit(solution)/shard_map/ppermute | solution.py:20
  53.0 9.3 %collective-permute-start.8 = (bf16[64,128]{1,0:T(8,128)(2,1)S(1)}, bf16[64,128]{1,0:T(8,128)(2,1)S(1)}, u32[]{:S(2)}, u32[]{:S(2)}) collective-permute-start(bf16[64,128]{1,0:T(8,128)(2,1)S(1)} %get-tuple-element.13), channel_id=1, source_target_pairs={{0,2},{1,3},{2,0},{3,1},{4,6},{5,7},{6,4},{7,5},{8,10},{9,11},{10,... | collective-permute-start | bytes 49160 | tf_op jit(solution)/shard_map/ppermute | solution.py:20
  53.1 9.2 %collective-permute-start.9 = (bf16[64,128]{1,0:T(8,128)(2,1)S(1)}, bf16[64,128]{1,0:T(8,128)(2,1)S(1)}, u32[]{:S(2)}, u32[]{:S(2)}) collective-permute-start(bf16[64,128]{1,0:T(8,128)(2,1)S(1)} %get-tuple-element.12), channel_id=1, source_target_pairs={{0,3},{1,2},{2,1},{3,0},{4,7},{5,6},{6,5},{7,4},{8,11},{9,10},{10,... | collective-permute-start | bytes 49160 | tf_op jit(solution)/shard_map/ppermute | solution.py:20
  55.1 0.8 copy-start.12
  55.9 6.7 %copy-start.3 = (f32[1,512,128]{2,1,0:T(8,128)S(1)}, f32[1,512,128]{2,1,0:T(8,128)}, u32[]{:S(2)}) copy-start(f32[1,512,128]{2,1,0:T(8,128)} %param.10) | copy-start | bytes 786436
  55.9 8.4 %copy-start.13 = (bf16[1,512,64]{1,2,0:T(8,128)(2,1)S(1)}, bf16[1,512,64]{1,2,0:T(8,128)(2,1)}, u32[]{:S(2)}) copy-start(bf16[1,512,64]{1,2,0:T(8,128)(2,1)} %param.14) | copy-start | bytes 196612
  64.3 32.3 %copy-start.4 = (bf16[512,128]{1,0:T(8,128)(2,1)}, bf16[512,128]{1,0:T(8,128)(2,1)S(1)}, u32[]{:S(2)}) copy-start(bf16[512,128]{1,0:T(8,128)(2,1)S(1)} %get-tuple-element.2.own) | copy-start | bytes 393220
  64.5 4.8 %collective-permute-start.14 = (bf16[64,128]{1,0:T(8,128)(2,1)S(1)}, bf16[64,128]{1,0:T(8,128)(2,1)S(1)}, u32[]{:S(2)}, u32[]{:S(2)}) collective-permute-start(bf16[64,128]{1,0:T(8,128)(2,1)S(1)} %bitcast.64), channel_id=1, source_target_pairs={{0,4},{4,8},{8,12},{12,0},{1,5},{5,9},{9,13},{13,1},{2,6},{6,10},{... | collective-permute-start | bytes 49160 | tf_op jit(solution)/shard_map/ppermute | solution.py:33
  64.5 4.7 %collective-permute-start.15 = (bf16[64,128]{1,0:T(8,128)(2,1)S(1)}, bf16[64,128]{1,0:T(8,128)(2,1)S(1)}, u32[]{:S(2)}, u32[]{:S(2)}) collective-permute-start(bf16[64,128]{1,0:T(8,128)(2,1)S(1)} %bitcast.65), channel_id=1, source_target_pairs={{0,12},{4,0},{8,4},{12,8},{1,13},{5,1},{9,5},{13,9},{2,14},{6,2},{... | collective-permute-start | bytes 49160 | tf_op jit(solution)/shard_map/ppermute | solution.py:33
  68.1 6.5 %collective-permute-start.16 = (bf16[64,128]{1,0:T(8,128)(2,1)S(1)}, bf16[64,128]{1,0:T(8,128)(2,1)S(1)}, u32[]{:S(2)}, u32[]{:S(2)}) collective-permute-start(bf16[64,128]{1,0:T(8,128)(2,1)S(1)} %bitcast.66), channel_id=1, source_target_pairs={{0,8},{4,12},{8,0},{12,4},{1,9},{5,13},{9,1},{13,5},{2,10},{6,14},... | collective-permute-start | bytes 49160 | tf_op jit(solution)/shard_map/ppermute | solution.py:33
  75.9 26.5 %copy-start.1 = (bf16[256,4096]{1,0:T(8,128)(2,1)S(1)}, bf16[256,4096]{1,0:T(8,128)(2,1)}, u32[]{:S(2)}) copy-start(bf16[256,4096]{1,0:T(8,128)(2,1)} %layout.1) | copy-start | bytes 6291460
  75.9 26.5 %all-to-all-start.1 = ((bf16[16,4,64,128]{3,2,1,0:T(8,128)(2,1)}), bf16[16,4,64,128]{3,2,1,0:T(8,128)(2,1)S(1)}, u32[]{:S(2)}, u32[]{:S(2)}) async-start(bf16[16,4,64,128]{3,2,1,0:T(8,128)(2,1)} %broadcast_in_dim.30), calls=%async_computation.1 | async-start | bytes 2097152 | tf_op jit(solution)/shard_map/all_to_all | solution.py:38
  79.7 2.9 %collective-permute-start.10 = (bf16[512,128]{1,0:T(8,128)(2,1)S(1)}, bf16[512,128]{1,0:T(8,128)(2,1)S(1)}, u32[]{:S(2)}, u32[]{:S(2)}) collective-permute-start(bf16[512,128]{1,0:T(8,128)(2,1)S(1)} %get-tuple-element.2.own), channel_id=1, source_target_pairs={{0,1},{1,0},{2,3},{3,2},{4,5},{5,4},{6,7},{7,6},{8,9},{9,8},{10,11... | collective-permute-start | bytes 393224 | tf_op jit(solution)/shard_map/ppermute | solution.py:20
  82.6 20.4 %copy-start.11 = (bf16[512,128]{1,0:T(8,128)(2,1)}, bf16[512,128]{1,0:T(8,128)(2,1)S(1)}, u32[]{:S(2)}) copy-start(bf16[512,128]{1,0:T(8,128)(2,1)S(1)} %collective-permute-done.10.other) | copy-start | bytes 393220
  82.6 13.2 %collective-permute-start.12 = (bf16[2,512,128]{2,1,0:T(8,128)(2,1)S(1)}, bf16[2,512,128]{2,1,0:T(8,128)(2,1)S(1)}, u32[]{:S(2)}, u32[]{:S(2)}) collective-permute-start(bf16[2,512,128]{2,1,0:T(8,128)(2,1)S(1)} %pad_maximum_fusion.3), channel_id=1, source_target_pairs={{0,4},{1,253},{2,6},{3,255},{4,8},{5,1},{6,10},{7,3},{8,12},{9,5},... | collective-permute-start | bytes 786440 | tf_op jit(solution)/shard_map/ppermute | solution.py:20
  89.7 9.0 %collective-permute-start.11 = (bf16[2,512,128]{2,1,0:T(8,128)(2,1)S(1)}, bf16[2,512,128]{2,1,0:T(8,128)(2,1)S(1)}, u32[]{:S(2)}, u32[]{:S(2)}) collective-permute-start(bf16[2,512,128]{2,1,0:T(8,128)(2,1)S(1)} %pad_maximum_fusion.3), channel_id=1, source_target_pairs={{0,2},{1,255},{2,4},{3,1},{4,6},{5,3},{6,8},{7,5},{8,10},{9,7},{10... | collective-permute-start | bytes 786440 | tf_op jit(solution)/shard_map/ppermute | solution.py:20
  95.8 0.7 copy-start.8
  98.7 0.8 copy-start.6
  99.5 6.4 %collective-permute-start.13 = (bf16[3,512,128]{2,1,0:T(8,128)(2,1)}, bf16[3,512,128]{2,1,0:T(8,128)(2,1)}, u32[]{:S(2)}, u32[]{:S(2)}) collective-permute-start(bf16[3,512,128]{2,1,0:T(8,128)(2,1)} %pad_maximum_fusion.1), channel_id=1, source_target_pairs={{0,1},{1,0},{2,3},{3,2},{4,5},{5,4},{6,7},{7,6},{8,9},{9,8},{10,11... | collective-permute-start | bytes 1179656 | tf_op jit(solution)/shard_map/ppermute | solution.py:20
  103.1 9.3 %collective-permute-start.17 = (bf16[64,128]{1,0:T(8,128)(2,1)S(1)}, bf16[64,128]{1,0:T(8,128)(2,1)S(1)}, u32[]{:S(2)}, u32[]{:S(2)}) collective-permute-start(bf16[64,128]{1,0:T(8,128)(2,1)S(1)} %get-tuple-element.8), channel_id=1, source_target_pairs={{0,1},{1,0},{2,3},{3,2},{4,5},{5,4},{6,7},{7,6},{8,9},{9,8},{10,11... | collective-permute-start | bytes 49160 | tf_op jit(solution)/shard_map/ppermute | solution.py:20
  104.2 8.2 %collective-permute-start.18 = (bf16[64,128]{1,0:T(8,128)(2,1)S(1)}, bf16[64,128]{1,0:T(8,128)(2,1)S(1)}, u32[]{:S(2)}, u32[]{:S(2)}) collective-permute-start(bf16[64,128]{1,0:T(8,128)(2,1)S(1)} %get-tuple-element.10), channel_id=1, source_target_pairs={{0,2},{1,3},{2,0},{3,1},{4,6},{5,7},{6,4},{7,5},{8,10},{9,11},{10,... | collective-permute-start | bytes 49160 | tf_op jit(solution)/shard_map/ppermute | solution.py:20
  104.2 8.2 %collective-permute-start.19 = (bf16[64,128]{1,0:T(8,128)(2,1)S(1)}, bf16[64,128]{1,0:T(8,128)(2,1)S(1)}, u32[]{:S(2)}, u32[]{:S(2)}) collective-permute-start(bf16[64,128]{1,0:T(8,128)(2,1)S(1)} %get-tuple-element.9), channel_id=1, source_target_pairs={{0,3},{1,2},{2,1},{3,0},{4,7},{5,6},{6,5},{7,4},{8,11},{9,10},{10,... | collective-permute-start | bytes 49160 | tf_op jit(solution)/shard_map/ppermute | solution.py:20
  105.9 6.7 %copy-start.2 = (f32[512,128]{1,0:T(8,128)S(1)}, f32[512,128]{1,0:T(8,128)}, u32[]{:S(2)}) copy-start(f32[512,128]{1,0:T(8,128)} %get-tuple-element.3.iterate) | copy-start | bytes 786436

commit v3 on v2

--- a/solution.py
+++ b/solution.py
@@ -13,6 +13,7 @@
 
 SLOTS = (8, 6, 7, 1, 0, 3, 2, 5, 4)
 ROW_STEPS = (0, -1, 1, 2)
+BLOCK = 128
 
 
 def moved(value, target):
@@ -65,15 +66,19 @@
         copy.start()
     for copy in copies:
         copy.wait()
-    for k in range(count):
-        tile_copies[k].wait()
-        product = scales[k] * jnp.dot(
-            tile_buf[k], window[slots[k]], preferred_element_type=jnp.float32
-        )
-        out[...] = product if k == 0 else out[...] + product
     for copy in vector_copies:
         copy.wait()
-    out[...] = right_buf[...] - (iterate_buf[...] + out[...])
+    for copy in tile_copies:
+        copy.wait()
+    for start in range(0, out.shape[0], BLOCK):
+        block = pl.ds(start, BLOCK)
+        total = None
+        for k in range(count):
+            product = scales[k] * jnp.dot(
+                tile_buf[k, block], window[slots[k]], preferred_element_type=jnp.float32
+            )
+            total = product if total is None else total + product
+        out[block] = right_buf[block] - (iterate_buf[block] + total)
 
 
 def base_residual(slots, scales, tiles, own, other, first, second, back, right, iterate):
@@ -152,6 +157,37 @@
     return own, other, first, second, back
 
 
+def in_row(coefs):
+    held = []
+    for steps in ROW_STEPS:
+        held.append(along_row(coefs, -steps) if steps else coefs)
+    return jnp.stack(held)
+
+
+def one_sweep(iterate, right_side, slots, scales, near_tiles, basis_in, basis_out, far_rows, targets):
+    coarse = iterate.astype(jnp.bfloat16)
+    coefs = jnp.einsum(
+        "lr,lc->rc", basis_in, coarse, preferred_element_type=jnp.float32
+    ).astype(jnp.bfloat16)
+    rank, cols = coefs.shape
+    held = in_row(coefs)
+    gathered = sent_to_all(held, "near")
+    base = base_residual(slots, scales, near_tiles, *halo(coarse), right_side, iterate)
+    partial_coefs = jnp.dot(
+        far_rows, gathered.reshape(-1, cols), preferred_element_type=jnp.float32
+    )
+    partial_coefs = partial_coefs.astype(jnp.bfloat16).reshape(targets, rank, cols)
+    far_coefs = partial_coefs[0].astype(jnp.float32)
+    for m in range(1, targets):
+        arrived = moved(partial_coefs[m], crossed(m))
+        far_coefs += arrived.astype(jnp.float32)
+    far_term = jnp.dot(
+        basis_out, far_coefs.astype(jnp.bfloat16), preferred_element_type=jnp.float32
+    )
+    residual = base - far_term
+    return iterate + damping * residual, residual
+
+
 def shards(
     right_side,
     start_guess,
@@ -174,36 +210,15 @@
     chosen = (side * offsets + REACH)[:, None] == places[None, :]
     slots = jnp.sum(jnp.where(chosen, jnp.array(SLOTS, jnp.int32)[None, :], 0), axis=1)
 
-    targets, sources, rank, _ = couplings.shape
+    targets, _, _, _ = couplings.shape
     place = jnp.stack([lax.axis_index(("near", "row")), lax.axis_index("row"), lax.axis_index("col")])
     far_rows = laid_out_couplings(place.astype(jnp.int32), couplings, clusters, row_count)
 
     residual = right_side
-    for sweep in range(ITERS):
-        coarse = iterate.astype(jnp.bfloat16)
-        coefs = jnp.einsum(
-            "lr,lc->rc", basis_in, coarse, preferred_element_type=jnp.float32
-        ).astype(jnp.bfloat16)
-        in_row = jnp.stack(
-            [along_row(coefs, -steps) if steps else coefs for steps in ROW_STEPS]
+    for _ in range(ITERS):
+        iterate, residual = one_sweep(
+            iterate, right_side, slots, scales, near_tiles, basis_in, basis_out, far_rows, targets
         )
-        gathered = sent_to_all(in_row, "near")
-        base = base_residual(slots, scales, near_tiles, *halo(coarse), right_side, iterate)
-        partial_coefs = (
-            jnp.dot(
-                far_rows, gathered.reshape(sources * rank, -1), preferred_element_type=jnp.float32
-            )
-            .astype(jnp.bfloat16)
-            .reshape(targets, rank, -1)
-        )
-        far_coefs = partial_coefs[0].astype(jnp.float32)
-        for m in range(1, targets):
-            far_coefs += moved(partial_coefs[m], crossed(m)).astype(jnp.float32)
-        far_term = jnp.dot(
-            basis_out, far_coefs.astype(jnp.bfloat16), preferred_element_type=jnp.float32
-        )
-        residual = base - far_term
-        iterate = iterate + damping * residual
     return (iterate[None], residual[None])
 
 

time: 115 us -> 113 us (0.983)
  Pallas kernels: 17.8 us -> 15.5 us
    pallas_call x2, Pallas kernels: 12.8 us -> 10.5 us  [base_residual(): pl.pallas_call(base_body, out_shape=jax.ShapeDtypeStruct((rows, cols), jn...]
  transfers between devices with their start and end apart: 22 -> 22, of which waited for: 8 -> 8; matrix products, arithmetic and copies ran while one was open for 5% -> 5% of each run, Pallas kernels for 16% -> 14%
where the time goes in v3:
time: 113 us; the launch traced here: 112 us
  starting transfers between devices  57.2 us (51%)
  waiting for transfers between devices  23.1 us (20%)
  Pallas kernels  15.5 us (14%)
  other arithmetic  6.89 us (6%)
  matrix products  4.63 us (4%)
  local copies, waits for them, and re-layouts  4.07 us (4%)
    ppermute x14, starting transfers between devices, moved(): lax.ppermute(value, ALL, [(source, target(source) % count) for source in...  31 us
    ppermute x6, starting transfers between devices, along_row(): lax.ppermute(value, 'row', [(source, (source + steps) % count) for source...  15.5 us
    ppermute x14, waiting for transfers between devices, moved(): lax.ppermute(value, ALL, [(source, target(source) % count) for source in...  14.9 us
    all_to_all x2, starting transfers between devices, sent_to_all(): return lax.all_to_all(copies, axis, split_axis=0, concat_axis=0, tiled=True)  10.7 us
    pallas_call x2, Pallas kernels, base_residual(): pl.pallas_call(base_body, out_shape=jax.ShapeDtypeStruct((rows, cols), jn...  10.5 us
    ppermute x6, waiting for transfers between devices, along_row(): lax.ppermute(value, 'row', [(source, (source + steps) % count) for source...  8.15 us
    pallas_call x1, Pallas kernels, laid_out_couplings(): pl.pallas_call(lambda *refs: layout_body(*refs, clusters=clusters, rows=r...  4.97 us
    dot_general x2, matrix products, one_sweep(): jnp.dot(far_rows, gathered.reshape(-1, cols), preferred_element_type=jnp....  2.98 us
  transfers between devices with their start and end apart: 22, of which 8 were waited for; matrix products, arithmetic and copies ran while one was open for 5% of the time, Pallas kernels for 14%

profile of v3, /device:TPU:1, one launch (start us, length us, event | category | flops | bytes accessed | tf_op | source)
XLA Modules:
  0.0 112.3 jit_solution(14106941903403663453)
XLA Ops:
  0.6 0.0 copy-start
  0.6 1.1 fusion.12
  1.8 1.0 convolution_convert_fusion.3
  2.8 3.9 %collective-permute-start.4 = (bf16[64,128]{1,0:T(8,128)(2,1)S(1)}, bf16[64,128]{1,0:T(8,128)(2,1)S(1)}, u32[]{:S(2)}, u32[]{:S(2)}) collective-permute-start(bf16[64,128]{1,0:T(8,128)(2,1)S(1)} %convolution_convert_fusion.3), channel_id=1, source_target_pairs={{0,4},{4,8},{8,12},{12,0},{1,5},{5,9},{9,13},{13,1},{2,6},{6,10},{... | collective-permute-start | bytes 49160 | tf_op jit(solution)/shard_map/ppermute | solution.py:34
  6.7 3.1 %collective-permute-start.5 = (bf16[64,128]{1,0:T(8,128)(2,1)S(1)}, bf16[64,128]{1,0:T(8,128)(2,1)S(1)}, u32[]{:S(2)}, u32[]{:S(2)}) collective-permute-start(bf16[64,128]{1,0:T(8,128)(2,1)S(1)} %convolution_convert_fusion.3), channel_id=1, source_target_pairs={{0,12},{4,0},{8,4},{12,8},{1,13},{5,1},{9,5},{13,9},{2,14},{6,2},{... | collective-permute-start | bytes 49160 | tf_op jit(solution)/shard_map/ppermute | solution.py:34
  9.8 4.4 %collective-permute-start.6 = (bf16[64,128]{1,0:T(8,128)(2,1)S(1)}, bf16[64,128]{1,0:T(8,128)(2,1)S(1)}, u32[]{:S(2)}, u32[]{:S(2)}) collective-permute-start(bf16[64,128]{1,0:T(8,128)(2,1)S(1)} %convolution_convert_fusion.3), channel_id=1, source_target_pairs={{0,8},{4,12},{8,0},{12,4},{1,9},{5,13},{9,1},{13,5},{2,10},{6,14},... | collective-permute-start | bytes 49160 | tf_op jit(solution)/shard_map/ppermute | solution.py:34
  14.2 0.0 collective-permute-done.4
  14.2 0.0 collective-permute-done.5
  14.2 2.1 %collective-permute-done.6 = bf16[64,128]{1,0:T(8,128)(2,1)S(1)} collective-permute-done((bf16[64,128]{1,0:T(8,128)(2,1)S(1)}, bf16[64,128]{1,0:T(8,128)(2,1)S(1)}, u32[]{:S(2)}, u32[]{:S(2)}) %collective-permute-start.6) | collective-permute-done | bytes 16416 | tf_op jit(solution)/shard_map/ppermute | solution.py:34
  16.3 1.3 %broadcast_in_dim.29 = bf16[16,4,64,128]{3,2,1,0:T(8,128)(2,1)} broadcast(bf16[4,64,128]{2,1,0:T(8,128)(2,1)S(1)} %pad_maximum_fusion.4), dimensions={1,2,3} | broadcast | bytes 1114112 | tf_op jit(solution)/shard_map/broadcast_in_dim | solution.py:38
  17.6 6.8 %all-to-all-start = ((bf16[16,4,64,128]{3,2,1,0:T(8,128)(2,1)}), bf16[16,4,64,128]{3,2,1,0:T(8,128)(2,1)S(1)}, u32[]{:S(2)}, u32[]{:S(2)}) async-start(bf16[16,4,64,128]{3,2,1,0:T(8,128)(2,1)} %broadcast_in_dim.29), calls=%async_computation | async-start | bytes 2097152 | tf_op jit(solution)/shard_map/all_to_all | solution.py:39
  24.3 2.5 %collective-permute-start = (bf16[512,128]{1,0:T(8,128)(2,1)S(1)}, bf16[512,128]{1,0:T(8,128)(2,1)S(1)}, u32[]{:S(2)}, u32[]{:S(2)}) collective-permute-start(bf16[512,128]{1,0:T(8,128)(2,1)S(1)} %get-tuple-element.7.own), channel_id=1, source_target_pairs={{0,1},{1,0},{2,3},{3,2},{4,5},{5,4},{6,7},{7,6},{8,9},{9,8},{10,11... | collective-permute-start | bytes 393224 | tf_op jit(solution)/shard_map/ppermute | solution.py:21
  26.8 0.6 pad_add_fusion.refs_0_
  27.4 5.0 %layout.1 = bf16[256,4096]{1,0:T(8,128)(2,1)} custom-call(s32[3]{0:T(128)} %pad_add_fusion.refs_0_, bf16[4,64,64,64]{3,2,1,0:T(8,128)(2,1)} %refs_1_.1), custom_call_target="tpu_custom_call" | custom-call | bytes 6291456 | tf_op jit(solution)/shard_map/layout/pallas_call | solution.py:135
  32.4 0.0 collective-permute-done.other
  32.4 7.2 %collective-permute-start.2 = (bf16[2,512,128]{2,1,0:T(8,128)(2,1)S(1)}, bf16[2,512,128]{2,1,0:T(8,128)(2,1)S(1)}, u32[]{:S(2)}, u32[]{:S(2)}) collective-permute-start(bf16[2,512,128]{2,1,0:T(8,128)(2,1)S(1)} %pad_maximum_fusion.2), channel_id=1, source_target_pairs={{0,4},{1,253},{2,6},{3,255},{4,8},{5,1},{6,10},{7,3},{8,12},{9,5},... | collective-permute-start | bytes 786440 | tf_op jit(solution)/shard_map/ppermute | solution.py:21
  39.7 1.9 %collective-permute-start.1 = (bf16[2,512,128]{2,1,0:T(8,128)(2,1)S(1)}, bf16[2,512,128]{2,1,0:T(8,128)(2,1)S(1)}, u32[]{:S(2)}, u32[]{:S(2)}) collective-permute-start(bf16[2,512,128]{2,1,0:T(8,128)(2,1)S(1)} %pad_maximum_fusion.2), channel_id=1, source_target_pairs={{0,2},{1,255},{2,4},{3,1},{4,6},{5,3},{6,8},{7,5},{8,10},{9,7},{10... | collective-permute-start | bytes 786440 | tf_op jit(solution)/shard_map/ppermute | solution.py:21
  41.6 0.7 select_reduce_fusion.slots
  42.4 3.4 %collective-permute-done.2.second = bf16[2,512,128]{2,1,0:T(8,128)(2,1)S(1)} collective-permute-done((bf16[2,512,128]{2,1,0:T(8,128)(2,1)S(1)}, bf16[2,512,128]{2,1,0:T(8,128)(2,1)S(1)}, u32[]{:S(2)}, u32[]{:S(2)}) %collective-permute-start.2) | collective-permute-done | bytes 262176 | tf_op jit(solution)/shard_map/ppermute | solution.py:21
  45.8 2.8 %collective-permute-done.1.first = bf16[2,512,128]{2,1,0:T(8,128)(2,1)S(1)} collective-permute-done((bf16[2,512,128]{2,1,0:T(8,128)(2,1)S(1)}, bf16[2,512,128]{2,1,0:T(8,128)(2,1)S(1)}, u32[]{:S(2)}, u32[]{:S(2)}) %collective-permute-start.1) | collective-permute-done | bytes 262176 | tf_op jit(solution)/shard_map/ppermute | solution.py:21
  48.7 1.9 %collective-permute-start.3 = (bf16[3,512,128]{2,1,0:T(8,128)(2,1)S(1)}, bf16[3,512,128]{2,1,0:T(8,128)(2,1)S(1)}, u32[]{:S(2)}, u32[]{:S(2)}) collective-permute-start(bf16[3,512,128]{2,1,0:T(8,128)(2,1)S(1)} %pad_maximum_fusion), channel_id=1, source_target_pairs={{0,1},{1,0},{2,3},{3,2},{4,5},{5,4},{6,7},{7,6},{8,9},{9,8},{10,11... | collective-permute-start | bytes 1179656 | tf_op jit(solution)/shard_map/ppermute | solution.py:21
  50.6 0.0 all-to-all-done
  50.6 2.3 %convolution_convert_fusion.1 = bf16[256,128]{1,0:T(8,128)(2,1)S(1)} fusion(bf16[256,4096]{1,0:T(8,128)(2,1)} %layout.1, bf16[4096,128]{1,0:T(8,128)(2,1)S(1)} %bitcast.55), kind=kOutput, calls=%fused_computation.3 | convolution fusion | flops 268468224 | bytes 3211264 | tf_op jit(solution)/shard_map/dot_general | solution.py:176
  52.9 0.1 collective-permute-start.7
  53.0 0.1 collective-permute-start.8
  53.1 2.0 %collective-permute-start.9 = (bf16[64,128]{1,0:T(8,128)(2,1)S(1)}, bf16[64,128]{1,0:T(8,128)(2,1)S(1)}, u32[]{:S(2)}, u32[]{:S(2)}) collective-permute-start(bf16[64,128]{1,0:T(8,128)(2,1)S(1)} %get-tuple-element.12), channel_id=1, source_target_pairs={{0,3},{1,2},{2,1},{3,0},{4,7},{5,6},{6,5},{7,4},{8,11},{9,10},{10,... | collective-permute-start | bytes 49160 | tf_op jit(solution)/shard_map/ppermute | solution.py:21
  55.1 0.0 collective-permute-done.3.back
  55.1 0.8 copy-done.12
  55.9 5.3 %near.2 = f32[512,128]{1,0:T(8,128)} custom-call(s32[7]{0:T(128)} %select_reduce_fusion.slots, f32[7]{0:T(128)} %bitcast.74, bf16[7,512,512]{2,1,0:T(8,128)(2,1)} %bitcast.53, bf16[512,128]{1,0:T(8,128)(2,1)} %copy-done.9, bf16[512,128]{1,0:T(8,128)(2,1)} %copy-done.10, bf16[2,512,128]{2,1,0:T(8,128)(2,1)} %copy-done.5, bf16[2,512,128]{2,1,0:T(8,128)(2,1)} %copy-done.7, ...), custom_call_target="tpu_custom_call" | custom-call | flops 469762048 | bytes 3670016 | tf_op jit(solution)/shard_map/near/pallas_call | solution.py:89
  61.2 0.0 collective-permute-done.7
  61.2 0.0 collective-permute-done.8
  61.2 0.0 collective-permute-done.9
  61.2 0.2 convolution_bitcast_fusion.1
  61.4 1.7 %fusion.11 = (bf16[512,128]{1,0:T(8,128)(2,1)S(1)}, f32[512,128]{1,0:T(8,128)}) fusion(f32[512,128]{1,0:T(8,128)} %near.2, f32[512,128]{1,0:T(8,128)S(1)} %convolution_bitcast_fusion.1, f32[1,512,128]{2,1,0:T(8,128)S(1)} %copy-done.3), kind=kLoop, calls=%fused_computation.35 | loop fusion | flops 262144 | bytes 1179648 | tf_op jit(solution)/shard_map/convert_element_type | solution.py:168
  63.1 0.2 convolution_convert_fusion.2
  63.3 0.1 collective-permute-start.14
  63.4 3.6 %collective-permute-start.15 = (bf16[64,128]{1,0:T(8,128)(2,1)S(1)}, bf16[64,128]{1,0:T(8,128)(2,1)S(1)}, u32[]{:S(2)}, u32[]{:S(2)}) collective-permute-start(bf16[64,128]{1,0:T(8,128)(2,1)S(1)} %bitcast.65), channel_id=1, source_target_pairs={{0,12},{4,0},{8,4},{12,8},{1,13},{5,1},{9,5},{13,9},{2,14},{6,2},{... | collective-permute-start | bytes 49160 | tf_op jit(solution)/shard_map/ppermute | solution.py:34
  67.0 0.5 collective-permute-start.16
  67.4 0.7 collective-permute-done.14
  68.1 0.0 collective-permute-done.15
  68.1 5.4 %collective-permute-done.16 = bf16[64,128]{1,0:T(8,128)(2,1)S(1)} collective-permute-done((bf16[64,128]{1,0:T(8,128)(2,1)S(1)}, bf16[64,128]{1,0:T(8,128)(2,1)S(1)}, u32[]{:S(2)}, u32[]{:S(2)}) %collective-permute-start.16) | collective-permute-done | bytes 16416 | tf_op jit(solution)/shard_map/ppermute | solution.py:34
  73.5 1.3 %broadcast_in_dim.30 = bf16[16,4,64,128]{3,2,1,0:T(8,128)(2,1)} broadcast(bf16[4,64,128]{2,1,0:T(8,128)(2,1)S(1)} %pad_maximum_fusion.5), dimensions={1,2,3} | broadcast | bytes 1114112 | tf_op jit(solution)/shard_map/broadcast_in_dim | solution.py:38
  74.7 4.0 %all-to-all-start.1 = ((bf16[16,4,64,128]{3,2,1,0:T(8,128)(2,1)}), bf16[16,4,64,128]{3,2,1,0:T(8,128)(2,1)S(1)}, u32[]{:S(2)}, u32[]{:S(2)}) async-start(bf16[16,4,64,128]{3,2,1,0:T(8,128)(2,1)} %broadcast_in_dim.30), calls=%async_computation.1 | async-start | bytes 2097152 | tf_op jit(solution)/shard_map/all_to_all | solution.py:39
  78.7 1.8 %collective-permute-start.10 = (bf16[512,128]{1,0:T(8,128)(2,1)S(1)}, bf16[512,128]{1,0:T(8,128)(2,1)S(1)}, u32[]{:S(2)}, u32[]{:S(2)}) collective-permute-start(bf16[512,128]{1,0:T(8,128)(2,1)S(1)} %get-tuple-element.2.own), channel_id=1, source_target_pairs={{0,1},{1,0},{2,3},{3,2},{4,5},{5,4},{6,7},{7,6},{8,9},{9,8},{10,11... | collective-permute-start | bytes 393224 | tf_op jit(solution)/shard_map/ppermute | solution.py:21
  80.5 1.0 collective-permute-done.10.other
  81.5 7.1 %collective-permute-start.12 = (bf16[2,512,128]{2,1,0:T(8,128)(2,1)S(1)}, bf16[2,512,128]{2,1,0:T(8,128)(2,1)S(1)}, u32[]{:S(2)}, u32[]{:S(2)}) collective-permute-start(bf16[2,512,128]{2,1,0:T(8,128)(2,1)S(1)} %pad_maximum_fusion.3), channel_id=1, source_target_pairs={{0,4},{1,253},{2,6},{3,255},{4,8},{5,1},{6,10},{7,3},{8,12},{9,5},... | collective-permute-start | bytes 786440 | tf_op jit(solution)/shard_map/ppermute | solution.py:21
  88.6 0.6 collective-permute-start.11
  89.1 5.5 %collective-permute-done.12.second = bf16[2,512,128]{2,1,0:T(8,128)(2,1)S(1)} collective-permute-done((bf16[2,512,128]{2,1,0:T(8,128)(2,1)S(1)}, bf16[2,512,128]{2,1,0:T(8,128)(2,1)S(1)}, u32[]{:S(2)}, u32[]{:S(2)}) %collective-permute-start.12) | collective-permute-done | bytes 262176 | tf_op jit(solution)/shard_map/ppermute | solution.py:21
  94.7 0.7 copy-done.8
  95.4 2.1 %collective-permute-done.11.first = bf16[2,512,128]{2,1,0:T(8,128)(2,1)S(1)} collective-permute-done((bf16[2,512,128]{2,1,0:T(8,128)(2,1)S(1)}, bf16[2,512,128]{2,1,0:T(8,128)(2,1)S(1)}, u32[]{:S(2)}, u32[]{:S(2)}) %collective-permute-start.11) | collective-permute-done | bytes 262176 | tf_op jit(solution)/shard_map/ppermute | solution.py:21
  97.6 0.8 pad_maximum_fusion.1
  98.4 2.7 %collective-permute-start.13 = (bf16[3,512,128]{2,1,0:T(8,128)(2,1)}, bf16[3,512,128]{2,1,0:T(8,128)(2,1)}, u32[]{:S(2)}, u32[]{:S(2)}) collective-permute-start(bf16[3,512,128]{2,1,0:T(8,128)(2,1)} %pad_maximum_fusion.1), channel_id=1, source_target_pairs={{0,1},{1,0},{2,3},{3,2},{4,5},{5,4},{6,7},{7,6},{8,9},{9,8},{10,11... | collective-permute-start | bytes 1179656 | tf_op jit(solution)/shard_map/ppermute | solution.py:21
  101.1 0.0 all-to-all-done.1
  101.1 0.7 convolution_convert_fusion
  101.8 1.4 %collective-permute-start.17 = (bf16[64,128]{1,0:T(8,128)(2,1)S(1)}, bf16[64,128]{1,0:T(8,128)(2,1)S(1)}, u32[]{:S(2)}, u32[]{:S(2)}) collective-permute-start(bf16[64,128]{1,0:T(8,128)(2,1)S(1)} %get-tuple-element.8), channel_id=1, source_target_pairs={{0,1},{1,0},{2,3},{3,2},{4,5},{5,4},{6,7},{7,6},{8,9},{9,8},{10,11... | collective-permute-start | bytes 49160 | tf_op jit(solution)/shard_map/ppermute | solution.py:21
  103.2 0.0 collective-permute-start.18
  103.2 1.7 %collective-permute-start.19 = (bf16[64,128]{1,0:T(8,128)(2,1)S(1)}, bf16[64,128]{1,0:T(8,128)(2,1)S(1)}, u32[]{:S(2)}, u32[]{:S(2)}) collective-permute-start(bf16[64,128]{1,0:T(8,128)(2,1)S(1)} %get-tuple-element.9), channel_id=1, source_target_pairs={{0,3},{1,2},{2,1},{3,0},{4,7},{5,6},{6,5},{7,4},{8,11},{9,10},{10,... | collective-permute-start | bytes 49160 | tf_op jit(solution)/shard_map/ppermute | solution.py:21
  104.9 0.0 collective-permute-done.13.back
  104.9 5.3 %near.3 = f32[512,128]{1,0:T(8,128)} custom-call(s32[7]{0:T(128)} %select_reduce_fusion.slots, f32[7]{0:T(128)} %bitcast.75, bf16[7,512,512]{2,1,0:T(8,128)(2,1)} %bitcast.54, bf16[512,128]{1,0:T(8,128)(2,1)} %copy-done.4, bf16[512,128]{1,0:T(8,128)(2,1)} %copy-done.11, bf16[2,512,128]{2,1,0:T(8,128)(2,1)} %copy-done.6, bf16[2,512,128]{2,1,0:T(8,128)(2,1)} %copy-done.8, ...), custom_call_target="tpu_custom_call" | custom-call | flops 469762048 | bytes 3670016 | tf_op jit(solution)/shard_map/near/pallas_call | solution.py:89
  110.2 0.0 collective-permute-done.17
  110.2 0.0 collective-permute-done.18
  110.2 0.0 collective-permute-done.19
  110.2 0.2 convolution_bitcast_fusion
  110.5 1.8 %subtract_bitcast_fusion = (f32[1,512,128]{2,1,0:T(8,128)}, f32[1,512,128]{2,1,0:T(8,128)}) fusion(f32[512,128]{1,0:T(8,128)} %near.3, f32[512,128]{1,0:T(8,128)S(1)} %convolution_bitcast_fusion, f32[512,128]{1,0:T(8,128)S(1)} %copy-done.2), kind=kLoop, calls=%fused_computation.13 | loop fusion | flops 196608 | bytes 1310720 | tf_op jit(solution)/shard_map/broadcast_in_dim | solution.py:222
  (39 shorter events, 0.2 us)
Async XLA Ops:
  0.6 60.6 %copy-start = (bf16[1,512,64]{1,2,0:T(8,128)(2,1)S(1)}, bf16[1,512,64]{1,2,0:T(8,128)(2,1)}, u32[]{:S(2)}) copy-start(bf16[1,512,64]{1,2,0:T(8,128)(2,1)} %param.15) | copy-start | bytes 196612
  1.7 30.7 %copy-start.9 = (bf16[512,128]{1,0:T(8,128)(2,1)}, bf16[512,128]{1,0:T(8,128)(2,1)S(1)}, u32[]{:S(2)}) copy-start(bf16[512,128]{1,0:T(8,128)(2,1)S(1)} %get-tuple-element.7.own) | copy-start | bytes 393220
  2.8 11.4 %collective-permute-start.4 = (bf16[64,128]{1,0:T(8,128)(2,1)S(1)}, bf16[64,128]{1,0:T(8,128)(2,1)S(1)}, u32[]{:S(2)}, u32[]{:S(2)}) collective-permute-start(bf16[64,128]{1,0:T(8,128)(2,1)S(1)} %convolution_convert_fusion.3), channel_id=1, source_target_pairs={{0,4},{4,8},{8,12},{12,0},{1,5},{5,9},{9,13},{13,1},{2,6},{6,10},{... | collective-permute-start | bytes 49160 | tf_op jit(solution)/shard_map/ppermute | solution.py:34
  6.7 7.5 %collective-permute-start.5 = (bf16[64,128]{1,0:T(8,128)(2,1)S(1)}, bf16[64,128]{1,0:T(8,128)(2,1)S(1)}, u32[]{:S(2)}, u32[]{:S(2)}) collective-permute-start(bf16[64,128]{1,0:T(8,128)(2,1)S(1)} %convolution_convert_fusion.3), channel_id=1, source_target_pairs={{0,12},{4,0},{8,4},{12,8},{1,13},{5,1},{9,5},{13,9},{2,14},{6,2},{... | collective-permute-start | bytes 49160 | tf_op jit(solution)/shard_map/ppermute | solution.py:34
  9.8 6.5 %collective-permute-start.6 = (bf16[64,128]{1,0:T(8,128)(2,1)S(1)}, bf16[64,128]{1,0:T(8,128)(2,1)S(1)}, u32[]{:S(2)}, u32[]{:S(2)}) collective-permute-start(bf16[64,128]{1,0:T(8,128)(2,1)S(1)} %convolution_convert_fusion.3), channel_id=1, source_target_pairs={{0,8},{4,12},{8,0},{12,4},{1,9},{5,13},{9,1},{13,5},{2,10},{6,14},... | collective-permute-start | bytes 49160 | tf_op jit(solution)/shard_map/ppermute | solution.py:34
  17.6 33.0 %all-to-all-start = ((bf16[16,4,64,128]{3,2,1,0:T(8,128)(2,1)}), bf16[16,4,64,128]{3,2,1,0:T(8,128)(2,1)S(1)}, u32[]{:S(2)}, u32[]{:S(2)}) async-start(bf16[16,4,64,128]{3,2,1,0:T(8,128)(2,1)} %broadcast_in_dim.29), calls=%async_computation | async-start | bytes 2097152 | tf_op jit(solution)/shard_map/all_to_all | solution.py:39
  24.3 8.1 %collective-permute-start = (bf16[512,128]{1,0:T(8,128)(2,1)S(1)}, bf16[512,128]{1,0:T(8,128)(2,1)S(1)}, u32[]{:S(2)}, u32[]{:S(2)}) collective-permute-start(bf16[512,128]{1,0:T(8,128)(2,1)S(1)} %get-tuple-element.7.own), channel_id=1, source_target_pairs={{0,1},{1,0},{2,3},{3,2},{4,5},{5,4},{6,7},{7,6},{8,9},{9,8},{10,11... | collective-permute-start | bytes 393224 | tf_op jit(solution)/shard_map/ppermute | solution.py:21
  27.4 14.2 %copy-start.14 = (s32[1,7]{1,0:T(1,128)S(1)}, s32[1,7]{1,0:T(1,128)}, u32[]{:S(2)}) copy-start(s32[1,7]{1,0:T(1,128)} %param.13) | copy-start | bytes 88
  27.4 14.2 %copy-start.15 = (s32[9]{0:T(128)S(1)}, s32[9]{0:T(128)}, u32[]{:S(2)}) copy-start(s32[9]{0:T(128)} %constant.54.clone) | copy-start | bytes 112
  32.4 20.4 %copy-start.10 = (bf16[512,128]{1,0:T(8,128)(2,1)}, bf16[512,128]{1,0:T(8,128)(2,1)S(1)}, u32[]{:S(2)}) copy-start(bf16[512,128]{1,0:T(8,128)(2,1)S(1)} %collective-permute-done.other) | copy-start | bytes 393220
  32.4 13.4 %collective-permute-start.2 = (bf16[2,512,128]{2,1,0:T(8,128)(2,1)S(1)}, bf16[2,512,128]{2,1,0:T(8,128)(2,1)S(1)}, u32[]{:S(2)}, u32[]{:S(2)}) collective-permute-start(bf16[2,512,128]{2,1,0:T(8,128)(2,1)S(1)} %pad_maximum_fusion.2), channel_id=1, source_target_pairs={{0,4},{1,253},{2,6},{3,255},{4,8},{5,1},{6,10},{7,3},{8,12},{9,5},... | collective-permute-start | bytes 786440 | tf_op jit(solution)/shard_map/ppermute | solution.py:21
  39.7 8.9 %collective-permute-start.1 = (bf16[2,512,128]{2,1,0:T(8,128)(2,1)S(1)}, bf16[2,512,128]{2,1,0:T(8,128)(2,1)S(1)}, u32[]{:S(2)}, u32[]{:S(2)}) collective-permute-start(bf16[2,512,128]{2,1,0:T(8,128)(2,1)S(1)} %pad_maximum_fusion.2), channel_id=1, source_target_pairs={{0,2},{1,255},{2,4},{3,1},{4,6},{5,3},{6,8},{7,5},{8,10},{9,7},{10... | collective-permute-start | bytes 786440 | tf_op jit(solution)/shard_map/ppermute | solution.py:21
  45.8 7.1 %copy-start.7 = (bf16[2,512,128]{2,1,0:T(8,128)(2,1)}, bf16[2,512,128]{2,1,0:T(8,128)(2,1)S(1)}, u32[]{:S(2)}) copy-start(bf16[2,512,128]{2,1,0:T(8,128)(2,1)S(1)} %collective-permute-done.2.second) | copy-start | bytes 786436
  48.6 6.5 %copy-start.5 = (bf16[2,512,128]{2,1,0:T(8,128)(2,1)}, bf16[2,512,128]{2,1,0:T(8,128)(2,1)S(1)}, u32[]{:S(2)}) copy-start(bf16[2,512,128]{2,1,0:T(8,128)(2,1)S(1)} %collective-permute-done.1.first) | copy-start | bytes 786436
  48.7 6.5 %collective-permute-start.3 = (bf16[3,512,128]{2,1,0:T(8,128)(2,1)S(1)}, bf16[3,512,128]{2,1,0:T(8,128)(2,1)S(1)}, u32[]{:S(2)}, u32[]{:S(2)}) collective-permute-start(bf16[3,512,128]{2,1,0:T(8,128)(2,1)S(1)} %pad_maximum_fusion), channel_id=1, source_target_pairs={{0,1},{1,0},{2,3},{3,2},{4,5},{5,4},{6,7},{7,6},{8,9},{9,8},{10,11... | collective-permute-start | bytes 1179656 | tf_op jit(solution)/shard_map/ppermute | solution.py:21
  52.9 8.3 %collective-permute-start.7 = (bf16[64,128]{1,0:T(8,128)(2,1)S(1)}, bf16[64,128]{1,0:T(8,128)(2,1)S(1)}, u32[]{:S(2)}, u32[]{:S(2)}) collective-permute-start(bf16[64,128]{1,0:T(8,128)(2,1)S(1)} %get-tuple-element.11), channel_id=1, source_target_pairs={{0,1},{1,0},{2,3},{3,2},{4,5},{5,4},{6,7},{7,6},{8,9},{9,8},{10,11... | collective-permute-start | bytes 49160 | tf_op jit(solution)/shard_map/ppermute | solution.py:21
  53.0 8.2 %collective-permute-start.8 = (bf16[64,128]{1,0:T(8,128)(2,1)S(1)}, bf16[64,128]{1,0:T(8,128)(2,1)S(1)}, u32[]{:S(2)}, u32[]{:S(2)}) collective-permute-start(bf16[64,128]{1,0:T(8,128)(2,1)S(1)} %get-tuple-element.13), channel_id=1, source_target_pairs={{0,2},{1,3},{2,0},{3,1},{4,6},{5,7},{6,4},{7,5},{8,10},{9,11},{10,... | collective-permute-start | bytes 49160 | tf_op jit(solution)/shard_map/ppermute | solution.py:21
  53.1 8.1 %collective-permute-start.9 = (bf16[64,128]{1,0:T(8,128)(2,1)S(1)}, bf16[64,128]{1,0:T(8,128)(2,1)S(1)}, u32[]{:S(2)}, u32[]{:S(2)}) collective-permute-start(bf16[64,128]{1,0:T(8,128)(2,1)S(1)} %get-tuple-element.12), channel_id=1, source_target_pairs={{0,3},{1,2},{2,1},{3,0},{4,7},{5,6},{6,5},{7,4},{8,11},{9,10},{10,... | collective-permute-start | bytes 49160 | tf_op jit(solution)/shard_map/ppermute | solution.py:21
  55.1 0.8 copy-start.12
  55.9 5.6 %copy-start.3 = (f32[1,512,128]{2,1,0:T(8,128)S(1)}, f32[1,512,128]{2,1,0:T(8,128)}, u32[]{:S(2)}) copy-start(f32[1,512,128]{2,1,0:T(8,128)} %param.10) | copy-start | bytes 786436
  55.9 7.3 %copy-start.13 = (bf16[1,512,64]{1,2,0:T(8,128)(2,1)S(1)}, bf16[1,512,64]{1,2,0:T(8,128)(2,1)}, u32[]{:S(2)}) copy-start(bf16[1,512,64]{1,2,0:T(8,128)(2,1)} %param.14) | copy-start | bytes 196612
  63.1 32.3 %copy-start.4 = (bf16[512,128]{1,0:T(8,128)(2,1)}, bf16[512,128]{1,0:T(8,128)(2,1)S(1)}, u32[]{:S(2)}) copy-start(bf16[512,128]{1,0:T(8,128)(2,1)S(1)} %get-tuple-element.2.own) | copy-start | bytes 393220
  63.3 4.8 %collective-permute-start.14 = (bf16[64,128]{1,0:T(8,128)(2,1)S(1)}, bf16[64,128]{1,0:T(8,128)(2,1)S(1)}, u32[]{:S(2)}, u32[]{:S(2)}) collective-permute-start(bf16[64,128]{1,0:T(8,128)(2,1)S(1)} %bitcast.64), channel_id=1, source_target_pairs={{0,4},{4,8},{8,12},{12,0},{1,5},{5,9},{9,13},{13,1},{2,6},{6,10},{... | collective-permute-start | bytes 49160 | tf_op jit(solution)/shard_map/ppermute | solution.py:34
  63.4 4.7 %collective-permute-start.15 = (bf16[64,128]{1,0:T(8,128)(2,1)S(1)}, bf16[64,128]{1,0:T(8,128)(2,1)S(1)}, u32[]{:S(2)}, u32[]{:S(2)}) collective-permute-start(bf16[64,128]{1,0:T(8,128)(2,1)S(1)} %bitcast.65), channel_id=1, source_target_pairs={{0,12},{4,0},{8,4},{12,8},{1,13},{5,1},{9,5},{13,9},{2,14},{6,2},{... | collective-permute-start | bytes 49160 | tf_op jit(solution)/shard_map/ppermute | solution.py:34
  67.0 6.5 %collective-permute-start.16 = (bf16[64,128]{1,0:T(8,128)(2,1)S(1)}, bf16[64,128]{1,0:T(8,128)(2,1)S(1)}, u32[]{:S(2)}, u32[]{:S(2)}) collective-permute-start(bf16[64,128]{1,0:T(8,128)(2,1)S(1)} %bitcast.66), channel_id=1, source_target_pairs={{0,8},{4,12},{8,0},{12,4},{1,9},{5,13},{9,1},{13,5},{2,10},{6,14},... | collective-permute-start | bytes 49160 | tf_op jit(solution)/shard_map/ppermute | solution.py:34
  74.7 26.4 %copy-start.1 = (bf16[256,4096]{1,0:T(8,128)(2,1)S(1)}, bf16[256,4096]{1,0:T(8,128)(2,1)}, u32[]{:S(2)}) copy-start(bf16[256,4096]{1,0:T(8,128)(2,1)} %layout.1) | copy-start | bytes 6291460
  74.7 26.4 %all-to-all-start.1 = ((bf16[16,4,64,128]{3,2,1,0:T(8,128)(2,1)}), bf16[16,4,64,128]{3,2,1,0:T(8,128)(2,1)S(1)}, u32[]{:S(2)}, u32[]{:S(2)}) async-start(bf16[16,4,64,128]{3,2,1,0:T(8,128)(2,1)} %broadcast_in_dim.30), calls=%async_computation.1 | async-start | bytes 2097152 | tf_op jit(solution)/shard_map/all_to_all | solution.py:39
  78.7 2.7 %collective-permute-start.10 = (bf16[512,128]{1,0:T(8,128)(2,1)S(1)}, bf16[512,128]{1,0:T(8,128)(2,1)S(1)}, u32[]{:S(2)}, u32[]{:S(2)}) collective-permute-start(bf16[512,128]{1,0:T(8,128)(2,1)S(1)} %get-tuple-element.2.own), channel_id=1, source_target_pairs={{0,1},{1,0},{2,3},{3,2},{4,5},{5,4},{6,7},{7,6},{8,9},{9,8},{10,11... | collective-permute-start | bytes 393224 | tf_op jit(solution)/shard_map/ppermute | solution.py:21
  81.4 20.3 %copy-start.11 = (bf16[512,128]{1,0:T(8,128)(2,1)}, bf16[512,128]{1,0:T(8,128)(2,1)S(1)}, u32[]{:S(2)}) copy-start(bf16[512,128]{1,0:T(8,128)(2,1)S(1)} %collective-permute-done.10.other) | copy-start | bytes 393220
  81.5 13.2 %collective-permute-start.12 = (bf16[2,512,128]{2,1,0:T(8,128)(2,1)S(1)}, bf16[2,512,128]{2,1,0:T(8,128)(2,1)S(1)}, u32[]{:S(2)}, u32[]{:S(2)}) collective-permute-start(bf16[2,512,128]{2,1,0:T(8,128)(2,1)S(1)} %pad_maximum_fusion.3), channel_id=1, source_target_pairs={{0,4},{1,253},{2,6},{3,255},{4,8},{5,1},{6,10},{7,3},{8,12},{9,5},... | collective-permute-start | bytes 786440 | tf_op jit(solution)/shard_map/ppermute | solution.py:21
  88.6 9.0 %collective-permute-start.11 = (bf16[2,512,128]{2,1,0:T(8,128)(2,1)S(1)}, bf16[2,512,128]{2,1,0:T(8,128)(2,1)S(1)}, u32[]{:S(2)}, u32[]{:S(2)}) collective-permute-start(bf16[2,512,128]{2,1,0:T(8,128)(2,1)S(1)} %pad_maximum_fusion.3), channel_id=1, source_target_pairs={{0,2},{1,255},{2,4},{3,1},{4,6},{5,3},{6,8},{7,5},{8,10},{9,7},{10... | collective-permute-start | bytes 786440 | tf_op jit(solution)/shard_map/ppermute | solution.py:21
  94.7 0.7 copy-start.8
  97.6 0.8 copy-start.6
  98.4 6.5 %collective-permute-start.13 = (bf16[3,512,128]{2,1,0:T(8,128)(2,1)}, bf16[3,512,128]{2,1,0:T(8,128)(2,1)}, u32[]{:S(2)}, u32[]{:S(2)}) collective-permute-start(bf16[3,512,128]{2,1,0:T(8,128)(2,1)} %pad_maximum_fusion.1), channel_id=1, source_target_pairs={{0,1},{1,0},{2,3},{3,2},{4,5},{5,4},{6,7},{7,6},{8,9},{9,8},{10,11... | collective-permute-start | bytes 1179656 | tf_op jit(solution)/shard_map/ppermute | solution.py:21
  101.8 8.4 %collective-permute-start.17 = (bf16[64,128]{1,0:T(8,128)(2,1)S(1)}, bf16[64,128]{1,0:T(8,128)(2,1)S(1)}, u32[]{:S(2)}, u32[]{:S(2)}) collective-permute-start(bf16[64,128]{1,0:T(8,128)(2,1)S(1)} %get-tuple-element.8), channel_id=1, source_target_pairs={{0,1},{1,0},{2,3},{3,2},{4,5},{5,4},{6,7},{7,6},{8,9},{9,8},{10,11... | collective-permute-start | bytes 49160 | tf_op jit(solution)/shard_map/ppermute | solution.py:21
  103.2 7.0 %collective-permute-start.18 = (bf16[64,128]{1,0:T(8,128)(2,1)S(1)}, bf16[64,128]{1,0:T(8,128)(2,1)S(1)}, u32[]{:S(2)}, u32[]{:S(2)}) collective-permute-start(bf16[64,128]{1,0:T(8,128)(2,1)S(1)} %get-tuple-element.10), channel_id=1, source_target_pairs={{0,2},{1,3},{2,0},{3,1},{4,6},{5,7},{6,4},{7,5},{8,10},{9,11},{10,... | collective-permute-start | bytes 49160 | tf_op jit(solution)/shard_map/ppermute | solution.py:21
  103.2 7.0 %collective-permute-start.19 = (bf16[64,128]{1,0:T(8,128)(2,1)S(1)}, bf16[64,128]{1,0:T(8,128)(2,1)S(1)}, u32[]{:S(2)}, u32[]{:S(2)}) collective-permute-start(bf16[64,128]{1,0:T(8,128)(2,1)S(1)} %get-tuple-element.9), channel_id=1, source_target_pairs={{0,3},{1,2},{2,1},{3,0},{4,7},{5,6},{6,5},{7,4},{8,11},{9,10},{10,... | collective-permute-start | bytes 49160 | tf_op jit(solution)/shard_map/ppermute | solution.py:21
  104.9 5.5 %copy-start.2 = (f32[512,128]{1,0:T(8,128)S(1)}, f32[512,128]{1,0:T(8,128)}, u32[]{:S(2)}) copy-start(f32[512,128]{1,0:T(8,128)} %get-tuple-element.3.iterate) | copy-start | bytes 786436
